TPU v7x, 512 devices: a whole 4x8x8 slice. The times are simulated.
512 devices in a mesh: seq: 16 (over z_lo, x), dp: 32 (over z_hi, y, core).
Axes of the slice: x: 4, y: 8, z: 8 (z_hi: 2, z_lo: 4; z = z_hi * 4 + z_lo), core: 2. Of those that a mesh axis runs over, the one named last changes fastest.
Arguments:
- inputs: bfloat16 [32, 3072, 2048], P('dp', 'seq'), may hold values from -6 to 6
- queries: bfloat16 [32, 3072, 2048], P('dp', 'seq'), may hold values from -6 to 6
- keys: bfloat16 [32, 3072, 512], P('dp', 'seq'), may hold values from -6 to 6
- value_matrix: bfloat16 [2048, 512], P('dp'), may hold values from -0.125 to 0.125
- out_grad: bfloat16 [32, 3072, 2048], P('dp', 'seq'), may hold values from -6 to 6
Outputs:
- query_gradient: bfloat16 [32, 3072, 2048], P('dp', 'seq')
- key_gradient: bfloat16 [32, 3072, 512], P('dp', 'seq')
- input_grad: bfloat16 [32, 3072, 2048], P('dp', 'seq')
- weight_grad: float32 [2048, 512], P('dp')
All inputs are finite; a program needn't handle non-finite values.
Results may differ from a plain program's by a relative error of at most 0.0058.
Values may be sent and summed in bfloat16 or wider, within the bound.
A program may use at most 64 MiB of HBM per device.

v0:
```python
import math

import jax
import jax.numpy as jnp
from jax import lax
from jax.sharding import Mesh
from jax.sharding import PartitionSpec as P

QUERY_HEADS = 32
KEY_VALUE_HEADS = 8
HEAD_WIDTH = 64
DP = ("dp_0", "dp_1", "dp_2")


def copy_for_each(array, axis):
    copies = jnp.broadcast_to(array, (lax.axis_size(axis), *array.shape))
    return lax.all_to_all(copies, axis, split_axis=0, concat_axis=0, tiled=True)


def laid_out(pieces, dim):
    shape = list(pieces.shape[1:])
    shape[dim] *= pieces.shape[0]
    return jnp.moveaxis(pieces, 0, dim).reshape(shape)


def whole_of(array, axes, dim):
    far, near = axes
    pieces = copy_for_each(copy_for_each(array, far), near)
    return laid_out(pieces.swapaxes(0, 1).reshape(-1, *array.shape), dim)


def in_one_piece(arrays, axis, dim, along):
    ends, at = ([], 0)
    for a in arrays[:-1]:
        at += a.shape[along]
        ends.append(at)
    both = jnp.concatenate(arrays, axis=along)
    return tuple(jnp.split(lax.all_gather(both, axis, axis=dim, tiled=True), ends, axis=along))


def cut_along(array, dim, devices):
    shape = array.shape
    pieces = array.reshape(*shape[:dim], devices, shape[dim] // devices, *shape[dim + 1 :])
    return jnp.moveaxis(pieces, dim, 0)


def summed_on_arrival(array, axis, dim):
    devices = lax.axis_size(axis)
    pieces = lax.all_to_all(cut_along(array, dim, devices), axis, 0, 0, tiled=True)
    return jnp.sum(pieces, axis=0)


def sum_in_two_steps(array, axes, dim):
    far, near = axes
    pieces = cut_along(array, dim, lax.axis_size(far))
    nearer = summed_on_arrival(pieces, near, dim + 1)
    arrived = lax.all_to_all(nearer, far, split_axis=0, concat_axis=0, tiled=True)
    return arrived.sum(axis=0)


def padded_to(lines, devices):
    spare = -len(lines) % devices
    return jnp.pad(lines, [(0, spare)] + [(0, 0)] * (lines.ndim - 1))


def collect(array, axis, dim):
    pieces = copy_for_each(array, axis)
    return laid_out(pieces, dim)


def total_of(array, axes):
    lines = array.reshape(-1, array.shape[-1])
    own = summed_on_arrival(padded_to(lines, lax.axis_size(axes)), axes, 0)
    whole = collect(own, axes, 0)
    return whole[: len(lines)].reshape(array.shape)


def body(inputs, queries, keys, value_matrix, out_grad):
    highest = lax.Precision.HIGHEST
    token_rows = inputs.shape[1]
    group_width = QUERY_HEADS // KEY_VALUE_HEADS
    width_kv = value_matrix.shape[1]
    flat_inputs = inputs[0]
    query_head_rows = queries[0].reshape(token_rows, KEY_VALUE_HEADS, group_width, HEAD_WIDTH)
    key_head_rows = keys[0].reshape(token_rows, KEY_VALUE_HEADS, HEAD_WIDTH)
    device_index = lax.axis_index("seq")
    position = device_index * token_rows + jnp.arange(token_rows, dtype=jnp.int32)
    row_scale = lax.rsqrt((position.astype(jnp.float32) + 1.0) * HEAD_WIDTH)
    scaled_output = (out_grad[0].astype(jnp.float32) * row_scale[:, None]).astype(jnp.bfloat16)
    scaled_output = scaled_output.reshape(token_rows, KEY_VALUE_HEADS, group_width, HEAD_WIDTH)
    whole_weight = whole_of(value_matrix, (("dp_0", "dp_1"), "dp_2"), 0)
    value_projected = jnp.dot(flat_inputs, whole_weight, preferred_element_type=jnp.float32)
    value_head_rows = value_projected.astype(jnp.bfloat16).reshape(
        token_rows, KEY_VALUE_HEADS, HEAD_WIDTH
    )
    key_state = jnp.einsum(
        "tgd,tge->gde", key_head_rows, value_head_rows, preferred_element_type=jnp.float32
    )
    query_state = jnp.einsum(
        "tghd,tghe->gde", query_head_rows, scaled_output, preferred_element_type=jnp.float32
    )
    block_list = in_one_piece((key_state[None], query_state[None]), "seq", 0, 1)
    indices = jnp.arange(block_list[0].shape[0], dtype=jnp.int32)
    earlier = (indices < device_index).astype(jnp.float32)[:, None, None, None]
    later = (indices > device_index).astype(jnp.float32)[:, None, None, None]
    prefix = jnp.sum(block_list[0] * earlier, 0)
    suffix = jnp.sum(block_list[1] * later, 0)
    causal = jnp.arange(token_rows)[:, None] >= jnp.arange(token_rows)[None, :]
    value_scores = jnp.where(
        causal,
        jnp.einsum(
            "tghe,sge->ghts", scaled_output, value_head_rows, preferred_element_type=jnp.float32
        ),
        0.0,
    )
    key_scores = jnp.where(
        causal,
        jnp.einsum(
            "tghd,sgd->ghts", query_head_rows, key_head_rows, preferred_element_type=jnp.float32
        ),
        0.0,
    )
    query_float = query_head_rows.astype(jnp.float32)
    scaled_float = scaled_output.astype(jnp.float32)
    keys_float = key_head_rows.astype(jnp.float32)
    values_float = value_head_rows.astype(jnp.float32)
    query_gradient = jnp.einsum("ghts,sgd->tghd", value_scores, keys_float, precision=highest)
    query_gradient = query_gradient + jnp.einsum(
        "gde,tghe->tghd", prefix, scaled_float, precision=highest
    )
    key_gradient = jnp.einsum("ghts,tghd->sgd", value_scores, query_float, precision=highest)
    key_gradient = key_gradient + jnp.einsum(
        "gde,sge->sgd", suffix, values_float, precision=highest
    )
    value_gradient = jnp.einsum("ghts,tghe->sge", key_scores, scaled_float, precision=highest)
    value_gradient = value_gradient + jnp.einsum(
        "gde,sgd->sge", suffix, keys_float, precision=highest
    )
    value_gradient = value_gradient.astype(jnp.bfloat16).reshape(token_rows, width_kv)
    input_grad = lax.dot_general(
        value_gradient, whole_weight, (((1,), (1,)), ((), ())), preferred_element_type=jnp.float32
    )
    shard_grad = sum_in_two_steps(
        lax.dot_general(
            flat_inputs,
            value_gradient,
            (((0,), (0,)), ((), ())),
            preferred_element_type=jnp.float32,
        ),
        (("dp_0", "dp_1"), "dp_2"),
        0,
    )
    summed_state = total_of(shard_grad, "seq")
    token_count = lax.axis_size("seq") * lax.axis_size(DP) * token_rows
    weight_grad = summed_state * (1.0 / math.sqrt(token_count))
    return (
        query_gradient.astype(jnp.bfloat16).reshape(1, token_rows, QUERY_HEADS * HEAD_WIDTH),
        key_gradient.astype(jnp.bfloat16).reshape(1, token_rows, KEY_VALUE_HEADS * HEAD_WIDTH),
        input_grad.astype(jnp.bfloat16).reshape(1, token_rows, inputs.shape[2]),
        weight_grad,
    )


def solution(mesh):
    torus = Mesh(mesh.devices.reshape(mesh.shape["seq"], 2, 8, 2), ("seq", "dp_0", "dp_1", "dp_2"))
    return jax.shard_map(
        body,
        mesh=torus,
        in_specs=(
            P(DP, "seq", None),
            P(DP, "seq", None),
            P(DP, "seq", None),
            P(DP, None),
            P(DP, "seq", None),
        ),
        out_specs=(P(DP, "seq", None), P(DP, "seq", None), P(DP, "seq", None), P(DP, None)),
        check_vma=False,
    )
```

profile of v0, /device:TPU:32, one launch (start us, length us, event | category | flops | bytes accessed | tf_op | source)
XLA Modules:
  0.0 323.6 jit_solution(15415824990251814934)
XLA Ops:
  7.2 2.1 broadcast_in_dim.33
  9.3 15.7 %all-to-all-start = ((bf16[16,64,512]{2,1,0:T(8,128)(2,1)}), bf16[16,64,512]{2,1,0:T(8,128)(2,1)}, u32[]{:S(2)}, u32[]{:S(2)}) async-start(bf16[16,64,512]{2,1,0:T(8,128)(2,1)} %broadcast_in_dim.33), calls=%async_computation | async-start | bytes 2097152 | tf_op jit(solution)/shard_map/all_to_all | solution.py:17
  26.6 1.4 copy.86
  29.2 26.9 %all-to-all-done = bf16[16,64,512]{2,1,0:T(8,128)(2,1)} async-done(((bf16[16,64,512]{2,1,0:T(8,128)(2,1)}), bf16[16,64,512]{2,1,0:T(8,128)(2,1)}, u32[]{:S(2)}, u32[]{:S(2)}) %all-to-all-start) | async-done | bytes 1048608 | tf_op jit(solution)/shard_map/all_to_all | solution.py:17
  56.1 1.5 broadcast_in_dim.34
  57.6 5.4 %all_to_all.30 = bf16[2,16,64,512]{3,2,1,0:T(8,128)(2,1)S(1)} all-to-all(bf16[2,16,64,512]{3,2,1,0:T(8,128)(2,1)S(1)} %broadcast_in_dim.34), channel_id=1, replica_groups=mesh['seq'=16,'dp_0'=2,'dp_1'=8,'dp_2'=2] {'dp_2'}, dimensions={0} | all-to-all | bytes 4194304 | tf_op jit(solution)/shard_map/all_to_all | solution.py:17
  63.2 1.4 copy-done.2
  67.1 1.8 pad_maximum_fusion
  68.9 2.0 copy.90
  72.1 4.7 %fusion.15 = f32[8,64,192]{2,1,0:T(8,128)} fusion(f32[8,192,192,4]{2,1,3,0:T(8,128)S(1)} %fusion.30, pred[192,192]{0,1:T(8,128)(4,1)S(1)} %iota_compare_fusion, bf16[192,8,4,64]{0,3,2,1:T(8,128)(2,1)S(1)} %bitcast.94, f32[192]{0:T(256)S(1)} %multiply_rsqrt_fusion), kind=kOutput, calls=%fused_computation.23 | convolution fusion | flops 908328960 | bytes 5935872 | tf_op jit(solution)/shard_map/ghts,tghe->sge/dot_general | solution.py:135
  76.8 97.6 %all-gather.2.cloned.1.call-done = f32[16,16,64,64]{3,2,1,0:T(8,128)} async-done(((f32[1,16,64,64]{3,2,1,0:T(8,128)}), f32[16,16,64,64]{3,2,1,0:T(8,128)}) %all-gather.2.cloned.1.call-update) | async-done | bytes 4194320 | tf_op jit(solution)/shard_map/all_gather | solution.py:38
  174.3 5.4 %fusion.3 = (f32[8,64,64]{2,1,0:T(8,128)S(1)}, f32[8,64,64]{2,1,0:T(8,128)}) fusion(f32[16,16,64,64]{3,2,1,0:T(8,128)} %all-gather.2.cloned.1.call-done, f32[16]{0:T(128)S(1)} %get-tuple-element.30, f32[16]{0:T(128)S(1)} %get-tuple-element.31), kind=kLoop, calls=%fused_computation.6 | loop fusion | flops 2031616 | bytes 4456576 | tf_op jit(solution)/shard_map/reduce_sum | solution.py:107
  181.6 2.7 convolution_bitcast_fusion
  184.2 5.4 %copy.96 = f32[2048,512]{1,0:T(8,128)} copy(f32[2048,512]{0,1:T(8,128)} %convolution_bitcast_fusion) | data formatting | bytes 8388608 | tf_op jit(solution)/shard_map/dot_general | solution.py:144
  189.6 2.8 copy.97
  192.4 8.2 %all_to_all.31 = f32[2,16,64,512]{3,2,1,0:T(8,128)} all-to-all(f32[2,16,64,512]{3,2,1,0:T(8,128)S(1)} %copy.97), channel_id=1, replica_groups=mesh['seq'=16,'dp_0'=2,'dp_1'=8,'dp_2'=2] {'dp_2'}, dimensions={0} | all-to-all | bytes 8388608 | tf_op jit(solution)/shard_map/all_to_all | solution.py:49
  200.5 4.2 %reduce_sum.47 = f32[16,64,512]{2,1,0:T(8,128)} reduce(f32[2,16,64,512]{3,2,1,0:T(8,128)} %all_to_all.31, f32[]{:T(128)} %constant.6.clone.1), dimensions={0}, to_apply=%region_2.3 | reduce | flops 524288 | bytes 6291460 | tf_op jit(solution)/shard_map/reduce_sum | solution.py:50
  204.8 10.1 %all-to-all-start.3 = ((f32[16,64,512]{2,1,0:T(8,128)}), f32[16,64,512]{2,1,0:T(8,128)}, u32[]{:S(2)}, u32[]{:S(2)}) async-start(f32[16,64,512]{2,1,0:T(8,128)} %reduce_sum.47), calls=%async_computation.3 | async-start | bytes 4194304 | tf_op jit(solution)/shard_map/all_to_all | solution.py:57
  215.8 2.7 copy-done.1
  218.5 4.7 %fusion.14 = f32[8,192,64]{1,2,0:T(8,128)} fusion(bf16[192,8,4,64]{0,3,2,1:T(8,128)(2,1)S(1)} %bitcast.102, f32[8,192,192,4]{2,1,3,0:T(8,128)S(1)} %fusion.24, pred[192,192]{0,1:T(8,128)(4,1)S(1)} %iota_compare_fusion), kind=kOutput, calls=%fused_computation.22 | convolution fusion | flops 907149312 | bytes 5935104 | tf_op jit(solution)/shard_map/ghts,tghd->sgd/dot_general | solution.py:131
  223.2 2.3 fusion.21
  225.5 57.5 %all-to-all-done.3 = f32[16,64,512]{2,1,0:T(8,128)} async-done(((f32[16,64,512]{2,1,0:T(8,128)}), f32[16,64,512]{2,1,0:T(8,128)}, u32[]{:S(2)}, u32[]{:S(2)}) %all-to-all-start.3) | async-done | bytes 2097184 | tf_op jit(solution)/shard_map/all_to_all | solution.py:57
  283.0 2.4 reduce_sum.48
  285.4 1.6 reshape.61
  287.0 4.2 %all-to-all-start.4 = ((f32[16,4,512]{2,1,0:T(4,128)}), f32[16,4,512]{2,1,0:T(4,128)}, u32[]{:S(2)}, u32[]{:S(2)}) async-start(f32[16,4,512]{2,1,0:T(4,128)} %reshape.61), calls=%async_computation.4 | async-start | bytes 262144 | tf_op jit(solution)/shard_map/all_to_all | solution.py:49
  291.2 6.7 %fusion.13 = bf16[192,8,4,64]{0,3,2,1:T(8,128)(2,1)} fusion(f32[8,192,4,64]{1,3,2,0:T(8,128)S(1)} %copy-done.4, bf16[192,8,64,1]{0,2,3,1:T(8,128)(2,1)S(1)} %bitcast.106, f32[8,192,192,4]{2,1,3,0:T(8,128)} %copy-done.1, pred[192,192]{0,1:T(8,128)(4,1)S(1)} %iota_compare_fusion), kind=kOutput, calls=%fused_computation.21 | convolution fusion | flops 907935744 | bytes 7311360 | tf_op jit(solution)/shard_map/ghts,sgd->tghd/dot_general | solution.py:127
  297.9 2.3 all-to-all-done.4
  301.8 5.3 %all-to-all-start.5 = ((f32[16,4,512]{2,1,0:T(4,128)}), f32[16,4,512]{2,1,0:T(4,128)S(1)}, u32[]{:S(2)}, u32[]{:S(2)}) async-start(f32[16,4,512]{2,1,0:T(4,128)} %broadcast_in_dim.38), calls=%async_computation.5 | async-start | bytes 262144 | tf_op jit(solution)/shard_map/all_to_all | solution.py:17
  307.1 2.2 fusion.16
  309.3 1.8 copy.100
  311.0 2.2 copy.99
  313.2 1.7 fusion.11
  (40 shorter events, 12.8 us)
Async XLA Ops:
  7.2 57.4 %copy-start = (bf16[1,192,2048]{2,1,0:T(8,128)(2,1)S(1)}, bf16[1,192,2048]{2,1,0:T(8,128)(2,1)}, u32[]{:S(2)}) copy-start(bf16[1,192,2048]{2,1,0:T(8,128)(2,1)} %param.5) | copy-start | bytes 2359300
  7.2 18.9 %copy-start.10 = (bf16[1,192,2048]{2,1,0:T(8,128)(2,1)S(1)}, bf16[1,192,2048]{2,1,0:T(8,128)(2,1)}, u32[]{:S(2)}) copy-start(bf16[1,192,2048]{2,1,0:T(8,128)(2,1)} %param.6) | copy-start | bytes 2359300
  9.3 46.9 %all-to-all-start = ((bf16[16,64,512]{2,1,0:T(8,128)(2,1)}), bf16[16,64,512]{2,1,0:T(8,128)(2,1)}, u32[]{:S(2)}, u32[]{:S(2)}) async-start(bf16[16,64,512]{2,1,0:T(8,128)(2,1)} %broadcast_in_dim.33), calls=%async_computation | async-start | bytes 2097152 | tf_op jit(solution)/shard_map/all_to_all | solution.py:17
  24.9 149.4 %all-gather.2.cloned.1.call-start = ((), (), s32[]{:S(2)}) async-start(), calls=%async_computation.6 | async-start | bytes 8912896 | tf_op jit(solution)/shard_map/all_gather | solution.py:38
  63.2 1.4 copy-start.2
  174.3 6.1 %copy-start.8 = (f32[8,64,192]{2,1,0:T(8,128)S(1)}, f32[8,64,192]{2,1,0:T(8,128)}, u32[]{:S(2)}) copy-start(f32[8,64,192]{2,1,0:T(8,128)} %fusion.15) | copy-start | bytes 1179652
  179.7 0.7 copy-start.7
  180.9 0.7 copy-start.5
  204.8 78.3 %all-to-all-start.3 = ((f32[16,64,512]{2,1,0:T(8,128)}), f32[16,64,512]{2,1,0:T(8,128)}, u32[]{:S(2)}, u32[]{:S(2)}) async-start(f32[16,64,512]{2,1,0:T(8,128)} %reduce_sum.47), calls=%async_computation.3 | async-start | bytes 4194304 | tf_op jit(solution)/shard_map/all_to_all | solution.py:57
  215.8 2.7 copy-start.1
  218.5 4.7 %copy-start.9 = (f32[8,64,64]{2,1,0:T(8,128)S(1)}, f32[8,64,64]{2,1,0:T(8,128)}, u32[]{:S(2)}) copy-start(f32[8,64,64]{2,1,0:T(8,128)} %get-tuple-element.29) | copy-start | bytes 393220
  225.5 65.7 %copy-start.4 = (f32[8,192,4,64]{1,3,2,0:T(8,128)S(1)}, f32[8,192,4,64]{1,3,2,0:T(8,128)}, u32[]{:S(2)}) copy-start(f32[8,192,4,64]{1,3,2,0:T(8,128)} %fusion.21) | copy-start | bytes 4718596
  287.0 13.1 %all-to-all-start.4 = ((f32[16,4,512]{2,1,0:T(4,128)}), f32[16,4,512]{2,1,0:T(4,128)}, u32[]{:S(2)}, u32[]{:S(2)}) async-start(f32[16,4,512]{2,1,0:T(4,128)} %reshape.61), calls=%async_computation.4 | async-start | bytes 262144 | tf_op jit(solution)/shard_map/all_to_all | solution.py:49
  297.9 15.3 %copy-start.3 = (bf16[2,16,64,512]{3,2,0,1:T(8,128)(2,1)S(1)}, bf16[2,16,64,512]{3,2,0,1:T(8,128)(2,1)}, u32[]{:S(2)}) copy-start(bf16[2,16,64,512]{3,2,0,1:T(8,128)(2,1)} %copy-done.2) | copy-start | bytes 6291460
  297.9 15.3 %copy-start.6 = (bf16[8,64,192]{2,1,0:T(8,128)(2,1)S(1)}, bf16[8,64,192]{2,1,0:T(8,128)(2,1)}, u32[]{:S(2)}) copy-start(bf16[8,64,192]{2,1,0:T(8,128)(2,1)} %copy-done.5) | copy-start | bytes 589828
  301.8 14.2 %all-to-all-start.5 = ((f32[16,4,512]{2,1,0:T(4,128)}), f32[16,4,512]{2,1,0:T(4,128)S(1)}, u32[]{:S(2)}, u32[]{:S(2)}) async-start(f32[16,4,512]{2,1,0:T(4,128)} %broadcast_in_dim.38), calls=%async_computation.5 | async-start | bytes 262144 | tf_op jit(solution)/shard_map/all_to_all | solution.py:17
Sparse Core Ops, SparseCore 0:
  71.1 103.1 all-gather.1
where the time goes:
time: 325 us; the launch traced here: 324 us
  waiting for transfers between devices  185 us (57%)
  starting transfers between devices  35.2 us (11%)
  local copies, waits for them, and re-layouts  30.3 us (9%)
  matrix products  29.9 us (9%)
  other arithmetic  14.8 us (5%)
  between operations  14.2 us (4%)
  blocking collectives  13.6 us (4%)
    all_gather x1, waiting for transfers between devices, in_one_piece(): lax.all_gather(both, axis, axis=dim, tiled=True)  97.6 us
    all_to_all x1, waiting for transfers between devices, sum_in_two_steps(): lax.all_to_all(nearer, far, split_axis=0, concat_axis=0, tiled=True)  57.5 us
    all_to_all x2, waiting for transfers between devices, copy_for_each(): return lax.all_to_all(copies, axis, split_axis=0, concat_axis=0, tiled=True)  28 us
    all_to_all x2, starting transfers between devices, copy_for_each(): return lax.all_to_all(copies, axis, split_axis=0, concat_axis=0, tiled=True)  21 us
    unnamed x27, local copies, waits for them, and re-layouts  12.4 us
    all_to_all x1, starting transfers between devices, sum_in_two_steps(): lax.all_to_all(nearer, far, split_axis=0, concat_axis=0, tiled=True)  10.1 us
    all_to_all x1, blocking collectives, summed_on_arrival(): lax.all_to_all(cut_along(array, dim, devices), axis, 0, 0, tiled=True)  8.16 us
    dot_general x1, matrix products, body(): jnp.einsum('ghts,sgd->tghd', value_scores, keys_float, precision=highest)  6.67 us
  transfers between devices with their start and end apart: 5, of which 5 were waited for; matrix products, arithmetic and copies ran while one was open for 10% of the time, Pallas kernels for 0%

commit v1 on v0

v1 whole, which is shorter than its diff:
```python
import math
from types import SimpleNamespace

import jax
import jax.numpy as jnp
from jax import lax
from jax.experimental import pallas as pl
from jax.experimental.pallas import tpu as pltpu
from jax.sharding import Mesh
from jax.sharding import PartitionSpec as P

TOKENS = 192
WIDTH = 2048
KV_WIDTH = 512
HEAD_WIDTH = 64
GROUPS = 8
SEQ = ("zl", "x")
DP = ("zh", "y", "c")
AXES = ("zl", "x", "zh", "y", "c")
BF = jnp.bfloat16
F32 = jnp.float32
MESH = pl.DeviceIdType.MESH
TOKEN_COUNT = 98304

VMEM_SCRATCH = dict(
    x=((TOKENS, WIDTH), BF),
    x2=((TOKENS, WIDTH), BF),
    q=((TOKENS, WIDTH), BF),
    o=((TOKENS, WIDTH), BF),
    s=((TOKENS, WIDTH), BF),
    k=((TOKENS, KV_WIDTH), BF),
    kd=((GROUPS, TOKENS, 128), BF),
    v=((TOKENS, KV_WIDTH), BF),
    wb=((32, 64, KV_WIDTH), BF),
    vgi=((TOKENS, KV_WIDTH), F32),
    vg=((2, TOKENS, 256), BF),
    vgp=((TOKENS, 256), BF),
    bd=((4, 128, 128), BF),
    qgi=((TOKENS, WIDTH), F32),
    st_s=((2, 4, 64, 128), BF),
    st_r1=((2, 4, 64, 128), BF),
    st_t=((2, 64, 128), BF),
    st_r2=((2, 4, 64, 128), BF),
    st_o=((2, 4, 64, 128), BF),
    st_r3=((2, 4, 64, 128), BF),
    ga=((4, 8, 2, 16, 256), BF),
    a1=((3, 8, 2, 16, 256), BF),
    a2s=((8, 2, 16, 256), BF),
    a2r=((7, 2, 16, 256), BF),
    a3s=((2, 16, 256), BF),
    a3r=((7, 16, 256), BF),
    gb=((8, 2, 4, 16, 128), BF),
    b1=((7, 2, 4, 16, 128), BF),
    b2s=((4, 2, 16, 128), BF),
    b2r=((3, 2, 16, 128), BF),
    b3s=((2, 16, 128), BF),
    b3r=((7, 16, 128), BF),
    gc=((2, 4, 8, 16, 128), BF),
    c1=((7, 8, 16, 128), BF),
    c2s=((8, 16, 128), BF),
    c2r=((7, 16, 128), BF),
    c3s=((16, 128), BF),
    c3r=((3, 16, 128), BF),
    fa=((16, 256), F32),
    fb=((16, 128), F32),
    fc=((16, 128), F32),
    wga=((8, 16, 256), F32),
    wgb=((8, 16, 128), F32),
    wgc=((8, 16, 128), F32),
    qgo=((TOKENS, WIDTH), BF),
    kgo=((TOKENS, KV_WIDTH), BF),
    igo=((TOKENS, WIDTH), BF),
    wgo=((64, KV_WIDTH), F32),
)
SEM_SCRATCH = dict(
    ld=(5,),
    out=(4,),
    wd_s=(1,),
    wd_r=(1,),
    wz_s=(1,),
    wz_r=(1,),
    wr_s=(1,),
    wr_r=(2, 2, 4),
    xx_s=(1,),
    xx_r=(1,),
    vv_s=(1,),
    vv_r=(1,),
    st_ss=(2, 3),
    st_rs=(2, 3),
    rs_s=(3, 4),
    rs_r=(3, 4),
)


def dot(a, b, dims=((1,), (0,))):
    return lax.dot_general(a, b, (dims, ((), ())), preferred_element_type=F32)


def take_bytes(ref, sem):
    pltpu.make_async_copy(ref, ref, sem).wait()


def kernel(x_h, q_h, k_h, w_h, o_h, qg_h, kg_h, ig_h, wg_h, *scratch):
    r = SimpleNamespace(**dict(zip([*VMEM_SCRATCH, *SEM_SCRATCH], scratch)))
    zl, x, zh, y, c = (lax.axis_index(a) for a in AXES)
    seq = zl * 4 + x

    def turned(value, step, size):
        return lax.rem(value + step, size)

    def send(src, dst, ssem, rsem, **where):
        pltpu.make_async_remote_copy(
            src, dst, ssem, rsem, device_id=where, device_id_type=MESH
        ).start()

    loads = [
        pltpu.make_async_copy(a, b, r.ld.at[i])
        for i, (a, b) in enumerate(
            [
                (w_h, r.wb.at[zh * 16 + y * 2 + c]),
                (o_h, r.o),
                (q_h, r.q),
                (k_h, r.k),
                (x_h, r.x),
            ]
        )
    ]
    for load in loads:
        load.start()

    peers = [dict(c=1 - c)]
    for d in range(1, 4):
        peers += [dict(x=turned(x, d, 4)), dict(x=turned(x, d, 4), c=1 - c)]
        peers += [dict(zl=turned(zl, d, 4)), dict(zl=turned(zl, d, 4), c=1 - c)]
    peers += [dict(zh=1 - zh, zl=turned(zl, d, 4)) for d in range(4)]
    peers += [dict(y=turned(y, d, 8)) for d in range(1, 8)]
    barrier = pltpu.get_barrier_semaphore()
    for peer in peers:
        pl.semaphore_signal(barrier, inc=1, device_id=peer, device_id_type=MESH)

    low64 = lax.broadcasted_iota(jnp.int32, (64, 128), 1) < 64
    low_rows = lax.broadcasted_iota(jnp.int32, (TOKENS, 128), 1) < 64
    one_low = jnp.where(low_rows, 1.0, 0.0)
    half_masks = [one_low.astype(BF), (1.0 - one_low).astype(BF)]

    loads[1].wait()
    loads[2].wait()

    @pl.loop(0, 4)
    def _(p):
        position = seq * TOKENS + lax.broadcasted_iota(jnp.int32, (TOKENS, 128), 0)
        scale = lax.rsqrt((position.astype(F32) + 1.0) * HEAD_WIDTH)
        folded = []
        for g in range(2):
            total = None
            for j in range(2):
                col = pl.ds(pl.multiple_of(p * 512 + g * 256 + j * 128, 128), 128)
                tile = (r.o[:, col].astype(F32) * scale).astype(BF)
                r.s[:, col] = tile
                m = dot(r.q[:, col], tile, ((0,), (0,)))
                total = m if total is None else total + m
            both = jnp.where(low64, total[:64], total[64:])
            folded.append(both + pltpu.roll(both, 64, 1))
        r.st_s[0, p] = jnp.where(low64, folded[0], folded[1]).astype(BF)

    loads[0].wait()
    pl.semaphore_wait(barrier, len(peers))

    def state_first(i):
        for d in range(1, 4):
            xp = turned(x, d, 4)
            send(r.st_s.at[i, xp], r.st_r1.at[i, x], r.st_ss.at[i, 0], r.st_rs.at[i, 0], x=xp)
        r.st_r1[i, x] = r.st_s[i, x]

    def state_second(i):
        take_bytes(r.st_r1.at[i, pl.ds(0, 3)], r.st_rs.at[i, 0])
        total = sum(r.st_r1[i, p].astype(F32) for p in range(4))
        r.st_t[i] = total.astype(BF)
        for d in range(1, 4):
            zp = turned(zl, d, 4)
            send(r.st_t.at[i], r.st_r2.at[i, zl], r.st_ss.at[i, 1], r.st_rs.at[i, 1], zl=zp)
        r.st_r2[i, zl] = r.st_t[i]

    def state_third(i):
        take_bytes(r.st_r2.at[i, pl.ds(0, 3)], r.st_rs.at[i, 1])
        rows = jnp.zeros((64, 128), F32)
        for z in range(4):
            counts = z > zl if i == 0 else z < zl
            rows = rows + jnp.where(counts, r.st_r2[i, z].astype(F32), 0.0)
        for xp in range(4):
            value = rows
            for p in range(xp + 1, 4) if i == 0 else range(xp):
                value = value + r.st_r1[i, p].astype(F32)
            r.st_o[i, xp] = value.astype(BF)
        for d in range(1, 4):
            xp = turned(x, d, 4)
            send(r.st_o.at[i, xp], r.st_r3.at[i, x], r.st_ss.at[i, 2], r.st_rs.at[i, 2], x=xp)
        r.st_r3[i, x] = r.st_o[i, x]

    def state_wait(i):
        take_bytes(r.st_r3.at[i, pl.ds(0, 3)], r.st_rs.at[i, 2])

    state_first(0)

    def shard_at(j, y_from):
        row = zh if j == 0 else 1 - zh
        return r.wb.at[row * 16 + y_from * 2 + c]

    def to_partner(piece):
        send(piece, piece, r.wd_s.at[0], r.wd_r.at[0], c=1 - c)

    def along(way, j, step, piece):
        yp = turned(y, 1 if way == 0 else 7, 8)
        send(piece, piece, r.wr_s.at[0], r.wr_r.at[way, j, step - 1], y=yp)

    def relay(step, j, ways=(0, 1)):
        for way in ways:
            piece = shard_at(j, turned(y, 8 - step if way == 0 else step, 8))
            take_bytes(piece, r.wr_r.at[way, j, step - 1])
            if step < 3 or (step == 3 and way == j):
                along(way, j, step + 1, piece)
            to_partner(piece)

    own = shard_at(0, y)
    along(0, 0, 1, own)
    along(1, 0, 1, own)
    send(own, own, r.wz_s.at[0], r.wz_r.at[0], zh=1 - zh)
    to_partner(own)
    loads[4].wait()
    send(r.x, r.x2, r.xx_s.at[0], r.xx_r.at[0], c=1 - c)

    loads[3].wait()
    t_row = lax.broadcasted_iota(jnp.int32, (TOKENS, TOKENS), 0)
    t_col = lax.broadcasted_iota(jnp.int32, (TOKENS, TOKENS), 1)

    def doubled(pair, g):
        pair = pair.astype(F32)
        other = pltpu.roll(pair, 64, 1)
        low, high = (pair, other) if g == 0 else (other, pair)
        return jnp.where(low_rows, low, high).astype(BF)

    def folded_pair(totals):
        ends = [t + pltpu.roll(t, 64, 1) for t in totals]
        return jnp.where(low_rows, ends[0], ends[1])

    @pl.loop(0, 4)
    def _(p):
        pair_col = pl.ds(pl.multiple_of(p * 128, 128), 128)
        totals = []
        for g in range(2):
            twice = doubled(r.k[:, pair_col], g)
            r.kd[p * 2 + g] = twice
            total = None
            for j in range(2):
                col = pl.ds(pl.multiple_of(p * 512 + g * 256 + j * 128, 128), 128)
                q_tile, s_tile = r.q[:, col], r.s[:, col]
                for half in half_masks:
                    scores = dot(twice, q_tile * half, ((1,), (1,)))
                    scores = jnp.where(t_col >= t_row, scores, 0.0).astype(BF)
                    part = dot(scores, s_tile * half)
                    total = part if total is None else total + part
            totals.append(total)
        r.vgi[:, pair_col] = folded_pair(totals)

    relay(1, 0)
    state_second(0)
    take_bytes(r.wb.at[0], r.wz_r.at[0])
    other = shard_at(1, y)
    along(0, 1, 1, other)
    along(1, 1, 1, other)
    to_partner(other)
    relay(2, 0)
    relay(1, 1)
    state_third(0)
    relay(3, 0)
    state_wait(0)

    for p in range(4):
        pair = r.st_r3[0, p].astype(F32)
        block = jnp.concatenate(
            [jnp.where(low64, pair, 0.0), jnp.where(low64, 0.0, pair)], axis=0
        ).astype(BF)
        r.bd[p] = block
        cols = slice(p * 128, p * 128 + 128)
        total = r.vgi[:, cols] + dot(r.k[:, cols], block)
        r.vg[p // 2, :, (p % 2) * 128 : (p % 2) * 128 + 128] = total.astype(BF)
    send(r.vg.at[1 - c], r.vgp, r.vv_s.at[0], r.vv_r.at[0], c=1 - c)
    take_bytes(r.x2, r.xx_r.at[0])
    relay(2, 1)
    take_bytes(r.vgp, r.vv_r.at[0])

    vg_own = r.vg[c]
    vg_other = r.vgp[...]
    for zp in range(2):

        @pl.loop(0, 8)
        def _(yp):
            col = pl.ds(pl.multiple_of(zp * 1024 + yp * 128, 128), 128)
            part = dot(r.x[:, col], vg_own, ((0,), (0,)))
            part = (part + dot(r.x2[:, col], vg_other, ((0,), (0,)))).astype(BF)
            for u in range(4):
                r.ga[u, yp, zp] = part[16 * u : 16 * u + 16]
                r.gb[yp, zp, u] = part[64 + 16 * u : 80 + 16 * u, :128]
                r.gc[zp, u, yp] = part[64 + 16 * u : 80 + 16 * u, 128:]

    z_peers = [(dh, dl) for dh in range(2) for dl in range(4)][1:]
    for d in range(1, 4):
        xp = turned(x, d, 4)
        send(r.ga.at[xp], r.a1.at[d - 1], r.rs_s.at[0, 0], r.rs_r.at[0, 0], x=xp)
    for d in range(1, 8):
        yp = turned(y, d, 8)
        send(r.gb.at[yp], r.b1.at[d - 1], r.rs_s.at[1, 0], r.rs_r.at[1, 0], y=yp)
    for n, (dh, dl) in enumerate(z_peers):
        hp, lp = turned(zh, dh, 2), turned(zl, dl, 4)
        send(r.gc.at[hp, lp], r.c1.at[n], r.rs_s.at[2, 0], r.rs_r.at[2, 0], zh=hp, zl=lp)

    relay(4, 0, (0,))
    relay(3, 1)
    relay(4, 1, (1,))
    take_bytes(r.wb.at[pl.ds(0, 16)], r.wd_r.at[0])

    whole = r.wb[...].reshape(WIDTH, KV_WIDTH)
    r.v[...] = dot(r.x[...], whole).astype(BF)
    for p in range(4):
        cols = slice(p * 128, p * 128 + 128)
        m = dot(r.v[:, cols], r.k[:, cols], ((0,), (0,)))
        r.st_s[1, p] = jnp.where(low64, m[:64], m[64:]).astype(BF)
    state_first(1)

    vg_whole = jnp.concatenate([r.vg[0], r.vg[1]], axis=1)

    @pl.loop(0, 8)
    def _(n):
        rows = r.wb[pl.ds(n * 4, 4)].reshape(256, KV_WIDTH)
        col = pl.ds(pl.multiple_of(n * 256, 256), 256)
        r.igo[:, col] = dot(vg_whole, rows, ((1,), (1,))).astype(BF)

    outs = [
        pltpu.make_async_copy(a, b, r.out.at[i])
        for i, (a, b) in enumerate([(r.igo, ig_h), (r.kgo, kg_h), (r.qgo, qg_h), (r.wgo, wg_h)])
    ]
    outs[0].start()

    state_second(1)

    @pl.loop(0, 4)
    def _(p):
        pair_col = pl.ds(pl.multiple_of(p * 128, 128), 128)
        totals = []
        for g in range(2):
            v_twice = doubled(r.v[:, pair_col], g)
            k_twice = r.kd[p * 2 + g]
            total = None
            for j in range(2):
                col = pl.ds(pl.multiple_of(p * 512 + g * 256 + j * 128, 128), 128)
                q_tile, s_tile = r.q[:, col], r.s[:, col]
                grads = []
                for half in half_masks:
                    s_half = s_tile * half
                    scores = dot(s_half, v_twice, ((1,), (1,)))
                    scores = jnp.where(t_row >= t_col, scores, 0.0).astype(BF)
                    grads.append(dot(scores, k_twice))
                    scores = dot(v_twice, s_half, ((1,), (1,)))
                    scores = jnp.where(t_col >= t_row, scores, 0.0).astype(BF)
                    part = dot(scores, q_tile * half)
                    total = part if total is None else total + part
                r.qgi[:, col] = jnp.where(low_rows, grads[0], grads[1])
            totals.append(total)
        total = folded_pair(totals) + dot(r.v[:, pair_col], r.bd[p], ((1,), (1,)))
        r.kgo[:, pair_col] = total.astype(BF)

    outs[1].start()

    take_bytes(r.a1, r.rs_r.at[0, 0])

    @pl.loop(0, 8)
    def _(yp):
        total = r.ga[x, yp].astype(F32)
        for d in range(3):
            total = total + r.a1[d, yp].astype(F32)
        r.a2s[yp] = total.astype(BF)

    for d in range(1, 8):
        yp = turned(y, d, 8)
        send(r.a2s.at[yp], r.a2r.at[d - 1], r.rs_s.at[0, 1], r.rs_r.at[0, 1], y=yp)

    take_bytes(r.b1, r.rs_r.at[1, 0])
    for zp in range(2):
        for u in range(4):
            total = r.gb[y, zp, u].astype(F32)
            for d in range(7):
                total = total + r.b1[d, zp, u].astype(F32)
            r.b2s[u, zp] = total.astype(BF)
    for d in range(1, 4):
        xp = turned(x, d, 4)
        send(r.b2s.at[xp], r.b2r.at[d - 1], r.rs_s.at[1, 1], r.rs_r.at[1, 1], x=xp)

    take_bytes(r.c1, r.rs_r.at[2, 0])
    for yp in range(8):
        total = r.gc[zh, zl, yp].astype(F32)
        for d in range(7):
            total = total + r.c1[d, yp].astype(F32)
        r.c2s[yp] = total.astype(BF)
    for d in range(1, 8):
        yp = turned(y, d, 8)
        send(r.c2s.at[yp], r.c2r.at[d - 1], r.rs_s.at[2, 1], r.rs_r.at[2, 1], y=yp)

    state_third(1)

    take_bytes(r.b2r, r.rs_r.at[1, 1])
    for zp in range(2):
        total = r.b2s[x, zp].astype(F32)
        for d in range(3):
            total = total + r.b2r[d, zp].astype(F32)
        r.b3s[zp] = total.astype(BF)
    for n, (dh, dl) in enumerate(z_peers):
        hp, lp = turned(zh, dh, 2), turned(zl, dl, 4)
        send(r.b3s.at[hp], r.b3r.at[n], r.rs_s.at[1, 2], r.rs_r.at[1, 2], zh=hp, zl=lp)

    take_bytes(r.a2r, r.rs_r.at[0, 1])
    for zp in range(2):
        total = r.a2s[y, zp].astype(F32)
        for d in range(7):
            total = total + r.a2r[d, zp].astype(F32)
        r.a3s[zp] = total.astype(BF)
    for n, (dh, dl) in enumerate(z_peers):
        hp, lp = turned(zh, dh, 2), turned(zl, dl, 4)
        send(r.a3s.at[hp], r.a3r.at[n], r.rs_s.at[0, 2], r.rs_r.at[0, 2], zh=hp, zl=lp)

    take_bytes(r.c2r, r.rs_r.at[2, 1])
    total = r.c2s[y].astype(F32)
    for d in range(7):
        total = total + r.c2r[d].astype(F32)
    r.c3s[...] = total.astype(BF)
    for d in range(1, 4):
        xp = turned(x, d, 4)
        send(r.c3s, r.c3r.at[d - 1], r.rs_s.at[2, 2], r.rs_r.at[2, 2], x=xp)

    state_wait(1)

    @pl.loop(0, 4)
    def _(p):
        pair = r.st_r3[1, p].astype(F32)
        other_way = pltpu.roll(pair, 64, 1)
        for g in range(2):
            low, high = (pair, other_way) if g == 0 else (other_way, pair)
            block = jnp.concatenate(
                [jnp.where(low64, low, 0.0), jnp.where(low64, 0.0, high)], axis=0
            ).astype(BF)
            for j in range(2):
                col = pl.ds(pl.multiple_of(p * 512 + g * 256 + j * 128, 128), 128)
                r.qgo[:, col] = (r.qgi[:, col] + dot(r.s[:, col], block)).astype(BF)

    outs[2].start()

    factor = 1.0 / math.sqrt(TOKEN_COUNT)
    here_x, here_zl = c * 4 + x, c * 4 + zl

    take_bytes(r.c3r, r.rs_r.at[2, 2])
    total = r.c3s[...].astype(F32)
    for d in range(3):
        total = total + r.c3r[d].astype(F32)
    r.fc[...] = total * factor
    take_bytes(r.b3r, r.rs_r.at[1, 2])
    total = r.b3s[zh].astype(F32)
    for d in range(7):
        total = total + r.b3r[d].astype(F32)
    r.fb[...] = total * factor
    take_bytes(r.a3r, r.rs_r.at[0, 2])
    total = r.a3s[zh].astype(F32)
    for d in range(7):
        total = total + r.a3r[d].astype(F32)
    r.fa[...] = total * factor

    def spread(src, dst, part, axis, at):
        target = 0 if part == 0 else 1
        for d in range(1, 4):
            where = {axis: turned(at, d, 4), "c": target}
            send(src, dst, r.rs_s.at[part, 3], r.rs_r.at[part, 3], **where)

        @pl.when(c != target)
        def _():
            send(src, dst, r.rs_s.at[part, 3], r.rs_r.at[part, 3], c=target)

    spread(r.fa, r.wga.at[here_x], 0, "x", x)
    spread(r.fb, r.wgb.at[here_x], 1, "x", x)
    spread(r.fc, r.wgc.at[here_zl], 2, "zl", zl)

    @pl.when(c == 0)
    def _():
        r.wga[here_x] = r.fa[...]
        take_bytes(r.wga.at[pl.ds(0, 7)], r.rs_r.at[0, 3])
        for n in range(8):
            cp, u = divmod(n, 4)
            r.wgo[16 * u : 16 * u + 16, 256 * cp : 256 * cp + 256] = r.wga[n]
        take_bytes(r.wga.at[pl.ds(0, 3)], r.rs_s.at[0, 3])
        take_bytes(r.wgb.at[pl.ds(0, 4)], r.rs_s.at[1, 3])
        take_bytes(r.wgc.at[pl.ds(0, 4)], r.rs_s.at[2, 3])

    @pl.when(c == 1)
    def _():
        r.wgb[here_x] = r.fb[...]
        r.wgc[here_zl] = r.fc[...]
        take_bytes(r.wgb.at[pl.ds(0, 7)], r.rs_r.at[1, 3])
        take_bytes(r.wgc.at[pl.ds(0, 7)], r.rs_r.at[2, 3])
        for n in range(8):
            cp, u = divmod(n, 4)
            r.wgo[16 * u : 16 * u + 16, 256 * cp : 256 * cp + 128] = r.wgb[n]
            r.wgo[16 * u : 16 * u + 16, 256 * cp + 128 : 256 * cp + 256] = r.wgc[n]
        take_bytes(r.wga.at[pl.ds(0, 4)], r.rs_s.at[0, 3])
        take_bytes(r.wgb.at[pl.ds(0, 3)], r.rs_s.at[1, 3])
        take_bytes(r.wgc.at[pl.ds(0, 3)], r.rs_s.at[2, 3])

    outs[3].start()

    take_bytes(r.wb.at[pl.ds(0, 16)], r.wd_s.at[0])
    take_bytes(r.wb.at[0], r.wz_s.at[0])
    take_bytes(r.wb.at[pl.ds(0, 14)], r.wr_s.at[0])
    take_bytes(r.x, r.xx_s.at[0])
    take_bytes(r.vgp, r.vv_s.at[0])
    for i in range(2):
        for n in range(3):
            take_bytes(r.st_s.at[i, pl.ds(0, 3)], r.st_ss.at[i, n])
    sent = [
        [r.a1, r.a2r, r.a3r],
        [r.b1, r.b2r, r.b3r],
        [r.c1, r.c2r, r.c3r],
    ]
    for part in range(3):
        for n in range(3):
            take_bytes(sent[part][n], r.rs_s.at[part, n])
    for out in outs:
        out.wait()


def body(inputs, queries, keys, value_matrix, out_grad):
    anywhere = pl.BlockSpec(memory_space=pl.ANY)
    query_gradient, key_gradient, input_grad, weight_grad = pl.pallas_call(
        kernel,
        out_shape=(
            jax.ShapeDtypeStruct((TOKENS, WIDTH), BF),
            jax.ShapeDtypeStruct((TOKENS, KV_WIDTH), BF),
            jax.ShapeDtypeStruct((TOKENS, WIDTH), BF),
            jax.ShapeDtypeStruct((64, KV_WIDTH), F32),
        ),
        in_specs=[anywhere] * 5,
        out_specs=(anywhere,) * 4,
        scratch_shapes=[pltpu.VMEM(*spec) for spec in VMEM_SCRATCH.values()]
        + [pltpu.SemaphoreType.DMA(shape) for shape in SEM_SCRATCH.values()],
        compiler_params=pltpu.CompilerParams(collective_id=0, has_side_effects=True),
    )(inputs[0], queries[0], keys[0], value_matrix, out_grad[0])
    return query_gradient[None], key_gradient[None], input_grad[None], weight_grad


def solution(mesh):
    torus = Mesh(mesh.devices.reshape(4, 4, 2, 8, 2), AXES)
    wide = P(DP, SEQ, None)
    return jax.shard_map(
        body,
        mesh=torus,
        in_specs=(wide, wide, wide, P(DP, None), wide),
        out_specs=(wide, wide, wide, P(DP, None)),
        check_vma=False,
    )
```

time: 325 us -> 75.4 us (0.23)
  the two profiles are of different devices: /device:TPU:32 before, /device:TPU:1 now
where the time goes in v1:
time: 75.4 us; the launch traced here: 75.2 us
  Pallas kernels  70 us (93%)
  local copies, waits for them, and re-layouts  4.53 us (6%)
    pallas_call x1, Pallas kernels, body(): pl.pallas_call(kernel, out_shape=(jax.ShapeDtypeStruct((TOKENS, WIDTH), B...  70 us
    unnamed x10, local copies, waits for them, and re-layouts  4.53 us

profile of v1, /device:TPU:1, one launch (start us, length us, event | category | flops | bytes accessed | tf_op | source)
XLA Modules:
  0.0 75.2 jit_solution(3321324089993859118)
XLA Ops:
  0.6 70.0 %shard_map.84 = (bf16[192,2048]{1,0:T(8,128)(2,1)}, bf16[192,512]{1,0:T(8,128)(2,1)}, bf16[192,2048]{1,0:T(8,128)(2,1)}, f32[64,512]{1,0:T(8,128)}) custom-call(bf16[192,2048]{1,0:T(8,128)(2,1)} %bitcast.9, bf16[192,2048]{1,0:T(8,128)(2,1)} %bitcast.10, bf16[192,512]{1,0:T(8,128)(2,1)} %bitcast.12, bf16[64,512]{1,0:T(8,128)(2,1)} %w_h.1, ...), custom_call_target="tpu_custom_call" | custom-call | tf_op jit(solution)/shard_map/pallas_call | solution.py:538
  70.7 0.0 copy-start.1
  70.7 0.0 copy-start
  70.7 2.2 %copy.13 = bf16[1,192,2048]{2,1,0:T(8,128)(2,1)} copy(bf16[1,192,2048]{2,1,0:T(8,128)(2,1)} %bitcast.8) | data formatting | bytes 1572864
  72.9 0.0 copy-done.1
  72.9 0.7 copy.14
  73.5 0.0 copy-done
  73.5 0.0 copy-start.2
  73.5 0.9 %copy.15 = bf16[1,192,2048]{2,1,0:T(8,128)(2,1)} copy(bf16[1,192,2048]{2,1,0:T(8,128)(2,1)S(1)} %bitcast.7) | data formatting | bytes 1572864
  74.4 0.1 copy-done.2
  74.6 0.7 copy.16
Async XLA Ops:
  70.7 2.2 %copy-start.1 = (bf16[192,512]{1,0:T(8,128)(2,1)S(1)}, bf16[192,512]{1,0:T(8,128)(2,1)}, u32[]{:S(2)}) copy-start(bf16[192,512]{1,0:T(8,128)(2,1)} %get-tuple-element.9) | copy-start | bytes 589828
  70.7 2.9 %copy-start = (bf16[192,2048]{1,0:T(8,128)(2,1)S(1)}, bf16[192,2048]{1,0:T(8,128)(2,1)}, u32[]{:S(2)}) copy-start(bf16[192,2048]{1,0:T(8,128)(2,1)} %get-tuple-element.10) | copy-start | bytes 2359300
  73.5 1.0 %copy-start.2 = (f32[64,512]{1,0:T(8,128)S(1)}, f32[64,512]{1,0:T(8,128)}, u32[]{:S(2)}) copy-start(f32[64,512]{1,0:T(8,128)} %get-tuple-element.19) | copy-start | bytes 393220

commit v2 on v1

--- a/solution.py
+++ b/solution.py
@@ -22,6 +22,12 @@
 MESH = pl.DeviceIdType.MESH
 TOKEN_COUNT = 98304
 
+OUTS = dict(
+    qgo=((TOKENS, WIDTH), BF),
+    kgo=((TOKENS, KV_WIDTH), BF),
+    igo=((TOKENS, WIDTH), BF),
+    wgo=((64, KV_WIDTH), F32),
+)
 VMEM_SCRATCH = dict(
     x=((TOKENS, WIDTH), BF),
     x2=((TOKENS, WIDTH), BF),
@@ -37,10 +43,14 @@
     vgp=((TOKENS, 256), BF),
     bd=((4, 128, 128), BF),
     qgi=((TOKENS, WIDTH), F32),
-    st_s=((2, 4, 64, 128), BF),
-    st_r1=((2, 4, 64, 128), BF),
-    st_t=((2, 64, 128), BF),
-    st_r2=((2, 4, 64, 128), BF),
+    xt=((WIDTH, TOKENS), BF),
+    x2t=((WIDTH, TOKENS), BF),
+    st_s=((2, 4, 64, 128), F32),
+    st_r1=((2, 4, 64, 128), F32),
+    st_t0=((64, 128), BF),
+    st_t1=((64, 128), F32),
+    st_r20=((4, 64, 128), BF),
+    st_r21=((4, 64, 128), F32),
     st_o=((2, 4, 64, 128), BF),
     st_r3=((2, 4, 64, 128), BF),
     ga=((4, 8, 2, 16, 256), BF),
@@ -67,14 +77,9 @@
     wga=((8, 16, 256), F32),
     wgb=((8, 16, 128), F32),
     wgc=((8, 16, 128), F32),
-    qgo=((TOKENS, WIDTH), BF),
-    kgo=((TOKENS, KV_WIDTH), BF),
-    igo=((TOKENS, WIDTH), BF),
-    wgo=((64, KV_WIDTH), F32),
 )
 SEM_SCRATCH = dict(
     ld=(5,),
-    out=(4,),
     wd_s=(1,),
     wd_r=(1,),
     wz_s=(1,),
@@ -96,12 +101,18 @@
     return lax.dot_general(a, b, (dims, ((), ())), preferred_element_type=F32)
 
 
+def span(start, size):
+    if isinstance(start, int):
+        return slice(start, start + size)
+    return pl.ds(pl.multiple_of(start, 128), size)
+
+
 def take_bytes(ref, sem):
     pltpu.make_async_copy(ref, ref, sem).wait()
 
 
-def kernel(x_h, q_h, k_h, w_h, o_h, qg_h, kg_h, ig_h, wg_h, *scratch):
-    r = SimpleNamespace(**dict(zip([*VMEM_SCRATCH, *SEM_SCRATCH], scratch)))
+def kernel(x_h, q_h, k_h, w_h, o_h, *rest):
+    r = SimpleNamespace(**dict(zip([*OUTS, *VMEM_SCRATCH, *SEM_SCRATCH], rest)))
     zl, x, zh, y, c = (lax.axis_index(a) for a in AXES)
     seq = zl * 4 + x
 
@@ -146,25 +157,26 @@
     loads[1].wait()
     loads[2].wait()
 
-    @pl.loop(0, 4)
-    def _(p):
+    for p in range(4):
         position = seq * TOKENS + lax.broadcasted_iota(jnp.int32, (TOKENS, 128), 0)
         scale = lax.rsqrt((position.astype(F32) + 1.0) * HEAD_WIDTH)
         folded = []
         for g in range(2):
             total = None
             for j in range(2):
-                col = pl.ds(pl.multiple_of(p * 512 + g * 256 + j * 128, 128), 128)
+                col = span(p * 512 + g * 256 + j * 128, 128)
                 tile = (r.o[:, col].astype(F32) * scale).astype(BF)
                 r.s[:, col] = tile
                 m = dot(r.q[:, col], tile, ((0,), (0,)))
                 total = m if total is None else total + m
             both = jnp.where(low64, total[:64], total[64:])
             folded.append(both + pltpu.roll(both, 64, 1))
-        r.st_s[0, p] = jnp.where(low64, folded[0], folded[1]).astype(BF)
+        r.st_s[0, p] = jnp.where(low64, folded[0], folded[1])
 
     loads[0].wait()
     pl.semaphore_wait(barrier, len(peers))
+
+    row_sum, row_sums = (r.st_t0, r.st_t1), (r.st_r20, r.st_r21)
 
     def state_first(i):
         for d in range(1, 4):
@@ -174,23 +186,23 @@
 
     def state_second(i):
         take_bytes(r.st_r1.at[i, pl.ds(0, 3)], r.st_rs.at[i, 0])
-        total = sum(r.st_r1[i, p].astype(F32) for p in range(4))
-        r.st_t[i] = total.astype(BF)
+        total = sum(r.st_r1[i, p] for p in range(4)).astype(row_sum[i].dtype)
+        row_sum[i][...] = total
         for d in range(1, 4):
             zp = turned(zl, d, 4)
-            send(r.st_t.at[i], r.st_r2.at[i, zl], r.st_ss.at[i, 1], r.st_rs.at[i, 1], zl=zp)
-        r.st_r2[i, zl] = r.st_t[i]
+            send(row_sum[i], row_sums[i].at[zl], r.st_ss.at[i, 1], r.st_rs.at[i, 1], zl=zp)
+        row_sums[i][zl] = total
 
     def state_third(i):
-        take_bytes(r.st_r2.at[i, pl.ds(0, 3)], r.st_rs.at[i, 1])
+        take_bytes(row_sums[i].at[pl.ds(0, 3)], r.st_rs.at[i, 1])
         rows = jnp.zeros((64, 128), F32)
         for z in range(4):
             counts = z > zl if i == 0 else z < zl
-            rows = rows + jnp.where(counts, r.st_r2[i, z].astype(F32), 0.0)
+            rows = rows + jnp.where(counts, row_sums[i][z].astype(F32), 0.0)
         for xp in range(4):
             value = rows
             for p in range(xp + 1, 4) if i == 0 else range(xp):
-                value = value + r.st_r1[i, p].astype(F32)
+                value = value + r.st_r1[i, p]
             r.st_o[i, xp] = value.astype(BF)
         for d in range(1, 4):
             xp = turned(x, d, 4)
@@ -224,7 +236,13 @@
     own = shard_at(0, y)
     along(0, 0, 1, own)
     along(1, 0, 1, own)
-    send(own, own, r.wz_s.at[0], r.wz_r.at[0], zh=1 - zh)
+    for edge, targets in ((3, (1, 0)), (0, (2, 3))):
+
+        @pl.when(zl == edge)
+        def _():
+            for target in targets:
+                send(own, own, r.wz_s.at[0], r.wz_r.at[0], zh=1 - zh, zl=target)
+
     to_partner(own)
     loads[4].wait()
     send(r.x, r.x2, r.xx_s.at[0], r.xx_r.at[0], c=1 - c)
@@ -243,16 +261,15 @@
         ends = [t + pltpu.roll(t, 64, 1) for t in totals]
         return jnp.where(low_rows, ends[0], ends[1])
 
-    @pl.loop(0, 4)
-    def _(p):
-        pair_col = pl.ds(pl.multiple_of(p * 128, 128), 128)
+    def key_scores(p):
+        pair_col = span(p * 128, 128)
         totals = []
         for g in range(2):
             twice = doubled(r.k[:, pair_col], g)
             r.kd[p * 2 + g] = twice
             total = None
             for j in range(2):
-                col = pl.ds(pl.multiple_of(p * 512 + g * 256 + j * 128, 128), 128)
+                col = span(p * 512 + g * 256 + j * 128, 128)
                 q_tile, s_tile = r.q[:, col], r.s[:, col]
                 for half in half_masks:
                     scores = dot(twice, q_tile * half, ((1,), (1,)))
@@ -262,17 +279,27 @@
             totals.append(total)
         r.vgi[:, pair_col] = folded_pair(totals)
 
+    def transpose(src, dst, first, last):
+        for n in range(first, last):
+            rows = span(n * 128, 128)
+            dst[rows, :] = src[:, rows].T
+
+    for p in range(3):
+        key_scores(p)
+    state_second(0)
+    key_scores(3)
     relay(1, 0)
-    state_second(0)
+    transpose(r.x, r.xt, 0, 16)
     take_bytes(r.wb.at[0], r.wz_r.at[0])
     other = shard_at(1, y)
     along(0, 1, 1, other)
     along(1, 1, 1, other)
     to_partner(other)
+    take_bytes(r.x2, r.xx_r.at[0])
+    transpose(r.x2, r.x2t, 0, 16)
+    state_third(0)
     relay(2, 0)
     relay(1, 1)
-    state_third(0)
-    relay(3, 0)
     state_wait(0)
 
     for p in range(4):
@@ -285,19 +312,14 @@
         total = r.vgi[:, cols] + dot(r.k[:, cols], block)
         r.vg[p // 2, :, (p % 2) * 128 : (p % 2) * 128 + 128] = total.astype(BF)
     send(r.vg.at[1 - c], r.vgp, r.vv_s.at[0], r.vv_r.at[0], c=1 - c)
-    take_bytes(r.x2, r.xx_r.at[0])
-    relay(2, 1)
     take_bytes(r.vgp, r.vv_r.at[0])
 
     vg_own = r.vg[c]
     vg_other = r.vgp[...]
     for zp in range(2):
-
-        @pl.loop(0, 8)
-        def _(yp):
-            col = pl.ds(pl.multiple_of(zp * 1024 + yp * 128, 128), 128)
-            part = dot(r.x[:, col], vg_own, ((0,), (0,)))
-            part = (part + dot(r.x2[:, col], vg_other, ((0,), (0,)))).astype(BF)
+        for yp in range(8):
+            rows = span(zp * 1024 + yp * 128, 128)
+            part = (dot(r.xt[rows, :], vg_own) + dot(r.x2t[rows, :], vg_other)).astype(BF)
             for u in range(4):
                 r.ga[u, yp, zp] = part[16 * u : 16 * u + 16]
                 r.gb[yp, zp, u] = part[64 + 16 * u : 80 + 16 * u, :128]
@@ -307,15 +329,17 @@
     for d in range(1, 4):
         xp = turned(x, d, 4)
         send(r.ga.at[xp], r.a1.at[d - 1], r.rs_s.at[0, 0], r.rs_r.at[0, 0], x=xp)
+    for n, (dh, dl) in enumerate(z_peers):
+        hp, lp = turned(zh, dh, 2), turned(zl, dl, 4)
+        send(r.gc.at[hp, lp], r.c1.at[n], r.rs_s.at[2, 0], r.rs_r.at[2, 0], zh=hp, zl=lp)
+
+    relay(3, 0)
+    relay(2, 1)
+    relay(4, 0, (0,))
+    relay(3, 1)
     for d in range(1, 8):
         yp = turned(y, d, 8)
         send(r.gb.at[yp], r.b1.at[d - 1], r.rs_s.at[1, 0], r.rs_r.at[1, 0], y=yp)
-    for n, (dh, dl) in enumerate(z_peers):
-        hp, lp = turned(zh, dh, 2), turned(zl, dl, 4)
-        send(r.gc.at[hp, lp], r.c1.at[n], r.rs_s.at[2, 0], r.rs_r.at[2, 0], zh=hp, zl=lp)
-
-    relay(4, 0, (0,))
-    relay(3, 1)
     relay(4, 1, (1,))
     take_bytes(r.wb.at[pl.ds(0, 16)], r.wd_r.at[0])
 
@@ -324,35 +348,18 @@
     for p in range(4):
         cols = slice(p * 128, p * 128 + 128)
         m = dot(r.v[:, cols], r.k[:, cols], ((0,), (0,)))
-        r.st_s[1, p] = jnp.where(low64, m[:64], m[64:]).astype(BF)
+        r.st_s[1, p] = jnp.where(low64, m[:64], m[64:])
     state_first(1)
 
-    vg_whole = jnp.concatenate([r.vg[0], r.vg[1]], axis=1)
-
-    @pl.loop(0, 8)
-    def _(n):
-        rows = r.wb[pl.ds(n * 4, 4)].reshape(256, KV_WIDTH)
-        col = pl.ds(pl.multiple_of(n * 256, 256), 256)
-        r.igo[:, col] = dot(vg_whole, rows, ((1,), (1,))).astype(BF)
-
-    outs = [
-        pltpu.make_async_copy(a, b, r.out.at[i])
-        for i, (a, b) in enumerate([(r.igo, ig_h), (r.kgo, kg_h), (r.qgo, qg_h), (r.wgo, wg_h)])
-    ]
-    outs[0].start()
-
-    state_second(1)
-
-    @pl.loop(0, 4)
-    def _(p):
-        pair_col = pl.ds(pl.multiple_of(p * 128, 128), 128)
+    def value_scores(p):
+        pair_col = span(p * 128, 128)
         totals = []
         for g in range(2):
             v_twice = doubled(r.v[:, pair_col], g)
             k_twice = r.kd[p * 2 + g]
             total = None
             for j in range(2):
-                col = pl.ds(pl.multiple_of(p * 512 + g * 256 + j * 128, 128), 128)
+                col = span(p * 512 + g * 256 + j * 128, 128)
                 q_tile, s_tile = r.q[:, col], r.s[:, col]
                 grads = []
                 for half in half_masks:
@@ -369,12 +376,9 @@
         total = folded_pair(totals) + dot(r.v[:, pair_col], r.bd[p], ((1,), (1,)))
         r.kgo[:, pair_col] = total.astype(BF)
 
-    outs[1].start()
-
     take_bytes(r.a1, r.rs_r.at[0, 0])
 
-    @pl.loop(0, 8)
-    def _(yp):
+    for yp in range(8):
         total = r.ga[x, yp].astype(F32)
         for d in range(3):
             total = total + r.a1[d, yp].astype(F32)
@@ -405,7 +409,11 @@
         yp = turned(y, d, 8)
         send(r.c2s.at[yp], r.c2r.at[d - 1], r.rs_s.at[2, 1], r.rs_r.at[2, 1], y=yp)
 
-    state_third(1)
+    value_scores(0)
+    value_scores(1)
+    state_second(1)
+    value_scores(2)
+    value_scores(3)
 
     take_bytes(r.b2r, r.rs_r.at[1, 1])
     for zp in range(2):
@@ -436,22 +444,14 @@
         xp = turned(x, d, 4)
         send(r.c3s, r.c3r.at[d - 1], r.rs_s.at[2, 2], r.rs_r.at[2, 2], x=xp)
 
-    state_wait(1)
-
-    @pl.loop(0, 4)
-    def _(p):
-        pair = r.st_r3[1, p].astype(F32)
-        other_way = pltpu.roll(pair, 64, 1)
-        for g in range(2):
-            low, high = (pair, other_way) if g == 0 else (other_way, pair)
-            block = jnp.concatenate(
-                [jnp.where(low64, low, 0.0), jnp.where(low64, 0.0, high)], axis=0
-            ).astype(BF)
-            for j in range(2):
-                col = pl.ds(pl.multiple_of(p * 512 + g * 256 + j * 128, 128), 128)
-                r.qgo[:, col] = (r.qgi[:, col] + dot(r.s[:, col], block)).astype(BF)
-
-    outs[2].start()
+    vg_whole = jnp.concatenate([r.vg[0], r.vg[1]], axis=1)
+
+    for n in range(8):
+        rows = r.wb[pl.ds(n * 4, 4)].reshape(256, KV_WIDTH)
+        col = span(n * 256, 256)
+        r.igo[:, col] = dot(vg_whole, rows, ((1,), (1,))).astype(BF)
+
+    state_third(1)
 
     factor = 1.0 / math.sqrt(TOKEN_COUNT)
     here_x, here_zl = c * 4 + x, c * 4 + zl
@@ -486,6 +486,21 @@
     spread(r.fb, r.wgb.at[here_x], 1, "x", x)
     spread(r.fc, r.wgc.at[here_zl], 2, "zl", zl)
 
+    state_wait(1)
+
+    for p in range(4):
+        pair = r.st_r3[1, p].astype(F32)
+        other_way = pltpu.roll(pair, 64, 1)
+        for g in range(2):
+            low, high = (pair, other_way) if g == 0 else (other_way, pair)
+            block = jnp.concatenate(
+                [jnp.where(low64, low, 0.0), jnp.where(low64, 0.0, high)], axis=0
+            ).astype(BF)
+            for j in range(2):
+                col = span(p * 512 + g * 256 + j * 128, 128)
+                r.qgo[:, col] = (r.qgi[:, col] + dot(r.s[:, col], block)).astype(BF)
+
+
     @pl.when(c == 0)
     def _():
         r.wga[here_x] = r.fa[...]
@@ -511,16 +526,20 @@
         take_bytes(r.wgb.at[pl.ds(0, 3)], r.rs_s.at[1, 3])
         take_bytes(r.wgc.at[pl.ds(0, 3)], r.rs_s.at[2, 3])
 
-    outs[3].start()
 
     take_bytes(r.wb.at[pl.ds(0, 16)], r.wd_s.at[0])
-    take_bytes(r.wb.at[0], r.wz_s.at[0])
+
+    @pl.when((zl == 0) | (zl == 3))
+    def _():
+        take_bytes(r.wb.at[pl.ds(0, 2)], r.wz_s.at[0])
+
     take_bytes(r.wb.at[pl.ds(0, 14)], r.wr_s.at[0])
     take_bytes(r.x, r.xx_s.at[0])
     take_bytes(r.vgp, r.vv_s.at[0])
     for i in range(2):
-        for n in range(3):
-            take_bytes(r.st_s.at[i, pl.ds(0, 3)], r.st_ss.at[i, n])
+        take_bytes(r.st_s.at[i, pl.ds(0, 3)], r.st_ss.at[i, 0])
+        take_bytes(row_sums[i].at[pl.ds(0, 3)], r.st_ss.at[i, 1])
+        take_bytes(r.st_o.at[i, pl.ds(0, 3)], r.st_ss.at[i, 2])
     sent = [
         [r.a1, r.a2r, r.a3r],
         [r.b1, r.b2r, r.b3r],
@@ -529,26 +548,45 @@
     for part in range(3):
         for n in range(3):
             take_bytes(sent[part][n], r.rs_s.at[part, n])
-    for out in outs:
-        out.wait()
+
+
+def put_out(*refs):
+    copies = [
+        pltpu.make_async_copy(refs[i], refs[i + 4], refs[8].at[i]) for i in range(4)
+    ]
+    for copy in copies:
+        copy.start()
+    for copy in copies:
+        copy.wait()
 
 
 def body(inputs, queries, keys, value_matrix, out_grad):
     anywhere = pl.BlockSpec(memory_space=pl.ANY)
-    query_gradient, key_gradient, input_grad, weight_grad = pl.pallas_call(
+    in_vmem = pl.BlockSpec(memory_space=pltpu.VMEM)
+    results = pl.pallas_call(
         kernel,
-        out_shape=(
-            jax.ShapeDtypeStruct((TOKENS, WIDTH), BF),
-            jax.ShapeDtypeStruct((TOKENS, KV_WIDTH), BF),
-            jax.ShapeDtypeStruct((TOKENS, WIDTH), BF),
-            jax.ShapeDtypeStruct((64, KV_WIDTH), F32),
-        ),
-        in_specs=[anywhere] * 5,
-        out_specs=(anywhere,) * 4,
+        out_shape=tuple(jax.ShapeDtypeStruct(*spec) for spec in OUTS.values()),
+        in_specs=[pl.BlockSpec(memory_space=pltpu.HBM)] * 5,
+        out_specs=(in_vmem,) * 4,
         scratch_shapes=[pltpu.VMEM(*spec) for spec in VMEM_SCRATCH.values()]
         + [pltpu.SemaphoreType.DMA(shape) for shape in SEM_SCRATCH.values()],
-        compiler_params=pltpu.CompilerParams(collective_id=0, has_side_effects=True),
-    )(inputs[0], queries[0], keys[0], value_matrix, out_grad[0])
+        compiler_params=pltpu.CompilerParams(
+            collective_id=0, has_side_effects=True, vmem_limit_bytes=40 << 20
+        ),
+    )(
+        *(
+            pltpu.with_memory_space_constraint(a, pltpu.HBM)
+            for a in (inputs[0], queries[0], keys[0], value_matrix, out_grad[0])
+        )
+    )
+    query_gradient, key_gradient, input_grad, weight_grad = pl.pallas_call(
+        put_out,
+        out_shape=tuple(jax.ShapeDtypeStruct(*spec) for spec in OUTS.values()),
+        in_specs=[in_vmem] * 4,
+        out_specs=(anywhere,) * 4,
+        scratch_shapes=[pltpu.SemaphoreType.DMA((4,))],
+        compiler_params=pltpu.CompilerParams(vmem_limit_bytes=8 << 20),
+    )(*results)
     return query_gradient[None], key_gradient[None], input_grad[None], weight_grad
 
 

time: 75.4 us -> 61.8 us (0.82)
  Pallas kernels: 70 us -> 61.1 us
  local copies, waits for them, and re-layouts: 4.53 us -> 0 us
    pallas_call x1 -> x2, Pallas kernels: 70 us -> 61.1 us  [the longest x1 59.8 us: body(): pl.pallas_call(kernel, out_shape=tuple((jax.ShapeDtypeStruct(*spec) for s...]
    unnamed x10 -> x0, local copies, waits for them, and re-layouts: 4.53 us -> none
where the time goes in v2:
time: 61.8 us; the launch traced here: 61.7 us
  Pallas kernels  61.1 us (99%)
  between operations  0.64 us (1%)
    pallas_call x1, Pallas kernels, body(): pl.pallas_call(kernel, out_shape=tuple((jax.ShapeDtypeStruct(*spec) for s...  59.8 us
    pallas_call x1, Pallas kernels, body(): pl.pallas_call(put_out, out_shape=tuple((jax.ShapeDtypeStruct(*spec) for...  1.28 us

profile of v2, /device:TPU:1, one launch (start us, length us, event | category | flops | bytes accessed | tf_op | source)
XLA Modules:
  0.0 61.7 jit_solution(4647665573643966646)
XLA Ops:
  0.6 59.8 %shard_map.84 = (bf16[192,2048]{1,0:T(8,128)(2,1)S(1)}, bf16[192,512]{1,0:T(8,128)(2,1)S(1)}, bf16[192,2048]{1,0:T(8,128)(2,1)S(1)}, f32[64,512]{1,0:T(8,128)S(1)}) custom-call(bf16[192,2048]{1,0:T(8,128)(2,1)} %bitcast.7, bf16[192,2048]{1,0:T(8,128)(2,1)} %bitcast.8, bf16[192,512]{1,0:T(8,128)(2,1)} %bitcast.10, bf16[64,512]{1,0:T(8,128)(2,1)} %w_h.1, ...), custom_call_target="tpu_custom_call" | custom-call | tf_op jit(solution)/shard_map/pallas_call | solution.py:566
  60.4 1.3 %shard_map.85 = (bf16[192,2048]{1,0:T(8,128)(2,1)}, bf16[192,512]{1,0:T(8,128)(2,1)}, bf16[192,2048]{1,0:T(8,128)(2,1)}, f32[64,512]{1,0:T(8,128)}) custom-call(bf16[192,2048]{1,0:T(8,128)(2,1)S(1)} %get-tuple-element.12.refs_0_, bf16[192,512]{1,0:T(8,128)(2,1)S(1)} %get-tuple-element.13.refs_1_, bf16[192,2048]{1,0:T(8,128)(2,1)S(1)} %get-tuple-element.14.refs_2_, ...), custom_call_target="tpu_custom_call" | custom-call | tf_op jit(solution)/shard_map/pallas_call | solution.py:582

commit v3 on v2

--- a/solution.py
+++ b/solution.py
@@ -35,7 +35,7 @@
     o=((TOKENS, WIDTH), BF),
     s=((TOKENS, WIDTH), BF),
     k=((TOKENS, KV_WIDTH), BF),
-    kd=((GROUPS, TOKENS, 128), BF),
+    kt=((KV_WIDTH, TOKENS), BF),
     v=((TOKENS, KV_WIDTH), BF),
     wb=((32, 64, KV_WIDTH), BF),
     vgi=((TOKENS, KV_WIDTH), F32),
@@ -48,9 +48,9 @@
     st_s=((2, 4, 64, 128), F32),
     st_r1=((2, 4, 64, 128), F32),
     st_t0=((64, 128), BF),
-    st_t1=((64, 128), F32),
+    st_t1=((64, 128), BF),
     st_r20=((4, 64, 128), BF),
-    st_r21=((4, 64, 128), F32),
+    st_r21=((4, 64, 128), BF),
     st_o=((2, 4, 64, 128), BF),
     st_r3=((2, 4, 64, 128), BF),
     ga=((4, 8, 2, 16, 256), BF),
@@ -81,11 +81,11 @@
 SEM_SCRATCH = dict(
     ld=(5,),
     wd_s=(1,),
-    wd_r=(1,),
+    wd_r=(2,),
     wz_s=(1,),
-    wz_r=(1,),
+    wz_r=(2,),
     wr_s=(1,),
-    wr_r=(2, 2, 4),
+    wr_r=(2, 2, 8),
     xx_s=(1,),
     xx_r=(1,),
     vv_s=(1,),
@@ -128,9 +128,9 @@
         pltpu.make_async_copy(a, b, r.ld.at[i])
         for i, (a, b) in enumerate(
             [
-                (w_h, r.wb.at[zh * 16 + y * 2 + c]),
                 (o_h, r.o),
                 (q_h, r.q),
+                (w_h, r.wb.at[zh * 16 + y * 2 + c]),
                 (k_h, r.k),
                 (x_h, r.x),
             ]
@@ -154,8 +154,8 @@
     one_low = jnp.where(low_rows, 1.0, 0.0)
     half_masks = [one_low.astype(BF), (1.0 - one_low).astype(BF)]
 
+    loads[0].wait()
     loads[1].wait()
-    loads[2].wait()
 
     for p in range(4):
         position = seq * TOKENS + lax.broadcasted_iota(jnp.int32, (TOKENS, 128), 0)
@@ -173,7 +173,7 @@
             folded.append(both + pltpu.roll(both, 64, 1))
         r.st_s[0, p] = jnp.where(low64, folded[0], folded[1])
 
-    loads[0].wait()
+    loads[2].wait()
     pl.semaphore_wait(barrier, len(peers))
 
     row_sum, row_sums = (r.st_t0, r.st_t1), (r.st_r20, r.st_r21)
@@ -214,36 +214,45 @@
 
     state_first(0)
 
-    def shard_at(j, y_from):
+    def shard_at(j, y_from, h):
         row = zh if j == 0 else 1 - zh
-        return r.wb.at[row * 16 + y_from * 2 + c]
-
-    def to_partner(piece):
-        send(piece, piece, r.wd_s.at[0], r.wd_r.at[0], c=1 - c)
-
-    def along(way, j, step, piece):
-        yp = turned(y, 1 if way == 0 else 7, 8)
-        send(piece, piece, r.wr_s.at[0], r.wr_r.at[way, j, step - 1], y=yp)
+        return r.wb.at[row * 16 + y_from * 2 + c, pl.ds(h * 32, 32)]
+
+    def to_partner(j, piece):
+        send(piece, piece, r.wd_s.at[0], r.wd_r.at[j], c=1 - c)
+
+    def along(way, j, step, h, piece, hops=1):
+        yp = turned(y, hops if way == 0 else 8 - hops, 8)
+        send(piece, piece, r.wr_s.at[0], r.wr_r.at[way, j, step - 1 + 4 * h], y=yp)
+
+    def begin(j, h):
+        piece = shard_at(j, y, h)
+        along(0, j, 1, h, piece)
+        along(1, j, 1, h, piece)
+        to_partner(j, piece)
 
     def relay(step, j, ways=(0, 1)):
-        for way in ways:
-            piece = shard_at(j, turned(y, 8 - step if way == 0 else step, 8))
-            take_bytes(piece, r.wr_r.at[way, j, step - 1])
-            if step < 3 or (step == 3 and way == j):
-                along(way, j, step + 1, piece)
-            to_partner(piece)
-
-    own = shard_at(0, y)
-    along(0, 0, 1, own)
-    along(1, 0, 1, own)
+        for h in range(2):
+            for way in ways:
+                piece = shard_at(j, turned(y, 8 - step if way == 0 else step, 8), h)
+                take_bytes(piece, r.wr_r.at[way, j, step - 1 + 4 * h])
+                if step < 3:
+                    along(way, j, step + 1, h, piece)
+                if step == 2 and way == j:
+                    along(way, j, 4, h, piece, 2)
+                to_partner(j, piece)
+
     for edge, targets in ((3, (1, 0)), (0, (2, 3))):
 
         @pl.when(zl == edge)
         def _():
-            for target in targets:
-                send(own, own, r.wz_s.at[0], r.wz_r.at[0], zh=1 - zh, zl=target)
-
-    to_partner(own)
+            for h in range(2):
+                piece = shard_at(0, y, h)
+                for target in targets:
+                    send(piece, piece, r.wz_s.at[0], r.wz_r.at[h], zh=1 - zh, zl=target)
+
+    begin(0, 0)
+    begin(0, 1)
     loads[4].wait()
     send(r.x, r.x2, r.xx_s.at[0], r.xx_r.at[0], c=1 - c)
 
@@ -263,10 +272,10 @@
 
     def key_scores(p):
         pair_col = span(p * 128, 128)
+        r.kt[pair_col, :] = r.k[:, pair_col].T
         totals = []
         for g in range(2):
             twice = doubled(r.k[:, pair_col], g)
-            r.kd[p * 2 + g] = twice
             total = None
             for j in range(2):
                 col = span(p * 512 + g * 256 + j * 128, 128)
@@ -287,18 +296,16 @@
     for p in range(3):
         key_scores(p)
     state_second(0)
+    relay(1, 0)
     key_scores(3)
-    relay(1, 0)
+    for h in range(2):
+        take_bytes(shard_at(1, y, h), r.wz_r.at[h])
+        begin(1, h)
     transpose(r.x, r.xt, 0, 16)
-    take_bytes(r.wb.at[0], r.wz_r.at[0])
-    other = shard_at(1, y)
-    along(0, 1, 1, other)
-    along(1, 1, 1, other)
-    to_partner(other)
+    relay(2, 0)
     take_bytes(r.x2, r.xx_r.at[0])
     transpose(r.x2, r.x2t, 0, 16)
     state_third(0)
-    relay(2, 0)
     relay(1, 1)
     state_wait(0)
 
@@ -312,6 +319,7 @@
         total = r.vgi[:, cols] + dot(r.k[:, cols], block)
         r.vg[p // 2, :, (p % 2) * 128 : (p % 2) * 128 + 128] = total.astype(BF)
     send(r.vg.at[1 - c], r.vgp, r.vv_s.at[0], r.vv_r.at[0], c=1 - c)
+    relay(3, 0)
     take_bytes(r.vgp, r.vv_r.at[0])
 
     vg_own = r.vg[c]
@@ -333,16 +341,28 @@
         hp, lp = turned(zh, dh, 2), turned(zl, dl, 4)
         send(r.gc.at[hp, lp], r.c1.at[n], r.rs_s.at[2, 0], r.rs_r.at[2, 0], zh=hp, zl=lp)
 
-    relay(3, 0)
     relay(2, 1)
-    relay(4, 0, (0,))
-    relay(3, 1)
     for d in range(1, 8):
         yp = turned(y, d, 8)
         send(r.gb.at[yp], r.b1.at[d - 1], r.rs_s.at[1, 0], r.rs_r.at[1, 0], y=yp)
+    relay(4, 0, (0,))
+    relay(3, 1)
     relay(4, 1, (1,))
-    take_bytes(r.wb.at[pl.ds(0, 16)], r.wd_r.at[0])
-
+
+    take_bytes(r.a1, r.rs_r.at[0, 0])
+
+    for yp in range(8):
+        total = r.ga[x, yp].astype(F32)
+        for d in range(3):
+            total = total + r.a1[d, yp].astype(F32)
+        r.a2s[yp] = total.astype(BF)
+
+    for d in range(1, 8):
+        yp = turned(y, d, 8)
+        send(r.a2s.at[yp], r.a2r.at[d - 1], r.rs_s.at[0, 1], r.rs_r.at[0, 1], y=yp)
+
+    take_bytes(r.wb.at[pl.ds(0, 8)], r.wd_r.at[0])
+    take_bytes(r.wb.at[pl.ds(0, 8)], r.wd_r.at[1])
     whole = r.wb[...].reshape(WIDTH, KV_WIDTH)
     r.v[...] = dot(r.x[...], whole).astype(BF)
     for p in range(4):
@@ -356,38 +376,24 @@
         totals = []
         for g in range(2):
             v_twice = doubled(r.v[:, pair_col], g)
-            k_twice = r.kd[p * 2 + g]
+            k_rows = r.kt[p * 128 + g * 64 : p * 128 + g * 64 + 64, :]
             total = None
             for j in range(2):
                 col = span(p * 512 + g * 256 + j * 128, 128)
                 q_tile, s_tile = r.q[:, col], r.s[:, col]
                 grads = []
                 for half in half_masks:
-                    s_half = s_tile * half
-                    scores = dot(s_half, v_twice, ((1,), (1,)))
-                    scores = jnp.where(t_row >= t_col, scores, 0.0).astype(BF)
-                    grads.append(dot(scores, k_twice))
-                    scores = dot(v_twice, s_half, ((1,), (1,)))
+                    scores = dot(v_twice, s_tile * half, ((1,), (1,)))
                     scores = jnp.where(t_col >= t_row, scores, 0.0).astype(BF)
+                    grads.append(dot(k_rows, scores))
                     part = dot(scores, q_tile * half)
                     total = part if total is None else total + part
-                r.qgi[:, col] = jnp.where(low_rows, grads[0], grads[1])
+                r.qgi[:, col] = jnp.concatenate(grads, axis=0).T
             totals.append(total)
         total = folded_pair(totals) + dot(r.v[:, pair_col], r.bd[p], ((1,), (1,)))
         r.kgo[:, pair_col] = total.astype(BF)
 
-    take_bytes(r.a1, r.rs_r.at[0, 0])
-
-    for yp in range(8):
-        total = r.ga[x, yp].astype(F32)
-        for d in range(3):
-            total = total + r.a1[d, yp].astype(F32)
-        r.a2s[yp] = total.astype(BF)
-
-    for d in range(1, 8):
-        yp = turned(y, d, 8)
-        send(r.a2s.at[yp], r.a2r.at[d - 1], r.rs_s.at[0, 1], r.rs_r.at[0, 1], y=yp)
-
+    value_scores(0)
     take_bytes(r.b1, r.rs_r.at[1, 0])
     for zp in range(2):
         for u in range(4):
@@ -409,12 +415,20 @@
         yp = turned(y, d, 8)
         send(r.c2s.at[yp], r.c2r.at[d - 1], r.rs_s.at[2, 1], r.rs_r.at[2, 1], y=yp)
 
-    value_scores(0)
     value_scores(1)
     state_second(1)
+
+    take_bytes(r.a2r, r.rs_r.at[0, 1])
+    for zp in range(2):
+        total = r.a2s[y, zp].astype(F32)
+        for d in range(7):
+            total = total + r.a2r[d, zp].astype(F32)
+        r.a3s[zp] = total.astype(BF)
+    for n, (dh, dl) in enumerate(z_peers):
+        hp, lp = turned(zh, dh, 2), turned(zl, dl, 4)
+        send(r.a3s.at[hp], r.a3r.at[n], r.rs_s.at[0, 2], r.rs_r.at[0, 2], zh=hp, zl=lp)
+
     value_scores(2)
-    value_scores(3)
-
     take_bytes(r.b2r, r.rs_r.at[1, 1])
     for zp in range(2):
         total = r.b2s[x, zp].astype(F32)
@@ -425,16 +439,6 @@
         hp, lp = turned(zh, dh, 2), turned(zl, dl, 4)
         send(r.b3s.at[hp], r.b3r.at[n], r.rs_s.at[1, 2], r.rs_r.at[1, 2], zh=hp, zl=lp)
 
-    take_bytes(r.a2r, r.rs_r.at[0, 1])
-    for zp in range(2):
-        total = r.a2s[y, zp].astype(F32)
-        for d in range(7):
-            total = total + r.a2r[d, zp].astype(F32)
-        r.a3s[zp] = total.astype(BF)
-    for n, (dh, dl) in enumerate(z_peers):
-        hp, lp = turned(zh, dh, 2), turned(zl, dl, 4)
-        send(r.a3s.at[hp], r.a3r.at[n], r.rs_s.at[0, 2], r.rs_r.at[0, 2], zh=hp, zl=lp)
-
     take_bytes(r.c2r, r.rs_r.at[2, 1])
     total = r.c2s[y].astype(F32)
     for d in range(7):
@@ -444,6 +448,9 @@
         xp = turned(x, d, 4)
         send(r.c3s, r.c3r.at[d - 1], r.rs_s.at[2, 2], r.rs_r.at[2, 2], x=xp)
 
+    value_scores(3)
+    state_third(1)
+
     vg_whole = jnp.concatenate([r.vg[0], r.vg[1]], axis=1)
 
     for n in range(8):
@@ -451,7 +458,6 @@
         col = span(n * 256, 256)
         r.igo[:, col] = dot(vg_whole, rows, ((1,), (1,))).astype(BF)
 
-    state_third(1)
 
     factor = 1.0 / math.sqrt(TOKEN_COUNT)
     here_x, here_zl = c * 4 + x, c * 4 + zl

time: 61.8 us -> 57.4 us (0.929)
  Pallas kernels: 61.1 us -> 56.6 us
    pallas_call x1, Pallas kernels: 59.8 us -> 55.3 us  [body(): pl.pallas_call(kernel, out_shape=tuple((jax.ShapeDtypeStruct(*spec) for s...]
where the time goes in v3:
time: 57.4 us; the launch traced here: 57.2 us
  Pallas kernels  56.6 us (99%)
  between operations  0.64 us (1%)
    pallas_call x1, Pallas kernels, body(): pl.pallas_call(kernel, out_shape=tuple((jax.ShapeDtypeStruct(*spec) for s...  55.3 us
    pallas_call x1, Pallas kernels, body(): pl.pallas_call(put_out, out_shape=tuple((jax.ShapeDtypeStruct(*spec) for...  1.28 us

profile of v3, /device:TPU:1, one launch (start us, length us, event | category | flops | bytes accessed | tf_op | source)
XLA Modules:
  0.0 57.2 jit_solution(13646906769718719882)
XLA Ops:
  0.6 55.3 %shard_map.84 = (bf16[192,2048]{1,0:T(8,128)(2,1)S(1)}, bf16[192,512]{1,0:T(8,128)(2,1)S(1)}, bf16[192,2048]{1,0:T(8,128)(2,1)S(1)}, f32[64,512]{1,0:T(8,128)S(1)}) custom-call(bf16[192,2048]{1,0:T(8,128)(2,1)} %bitcast.7, bf16[192,2048]{1,0:T(8,128)(2,1)} %bitcast.8, bf16[192,512]{1,0:T(8,128)(2,1)} %bitcast.10, bf16[64,512]{1,0:T(8,128)(2,1)} %w_h.1, ...), custom_call_target="tpu_custom_call" | custom-call | tf_op jit(solution)/shard_map/pallas_call | solution.py:572
  56.0 1.3 %shard_map.85 = (bf16[192,2048]{1,0:T(8,128)(2,1)}, bf16[192,512]{1,0:T(8,128)(2,1)}, bf16[192,2048]{1,0:T(8,128)(2,1)}, f32[64,512]{1,0:T(8,128)}) custom-call(bf16[192,2048]{1,0:T(8,128)(2,1)S(1)} %get-tuple-element.12.refs_0_, bf16[192,512]{1,0:T(8,128)(2,1)S(1)} %get-tuple-element.13.refs_1_, bf16[192,2048]{1,0:T(8,128)(2,1)S(1)} %get-tuple-element.14.refs_2_, ...), custom_call_target="tpu_custom_call" | custom-call | tf_op jit(solution)/shard_map/pallas_call | solution.py:588

commit v4 on v3

--- a/solution.py
+++ b/solution.py
@@ -320,6 +320,7 @@
         r.vg[p // 2, :, (p % 2) * 128 : (p % 2) * 128 + 128] = total.astype(BF)
     send(r.vg.at[1 - c], r.vgp, r.vv_s.at[0], r.vv_r.at[0], c=1 - c)
     relay(3, 0)
+    relay(2, 1)
     take_bytes(r.vgp, r.vv_r.at[0])
 
     vg_own = r.vg[c]
@@ -341,7 +342,6 @@
         hp, lp = turned(zh, dh, 2), turned(zl, dl, 4)
         send(r.gc.at[hp, lp], r.c1.at[n], r.rs_s.at[2, 0], r.rs_r.at[2, 0], zh=hp, zl=lp)
 
-    relay(2, 1)
     for d in range(1, 8):
         yp = turned(y, d, 8)
         send(r.gb.at[yp], r.b1.at[d - 1], r.rs_s.at[1, 0], r.rs_r.at[1, 0], y=yp)
@@ -416,6 +416,7 @@
         send(r.c2s.at[yp], r.c2r.at[d - 1], r.rs_s.at[2, 1], r.rs_r.at[2, 1], y=yp)
 
     value_scores(1)
+    value_scores(2)
     state_second(1)
 
     take_bytes(r.a2r, r.rs_r.at[0, 1])
@@ -428,7 +429,6 @@
         hp, lp = turned(zh, dh, 2), turned(zl, dl, 4)
         send(r.a3s.at[hp], r.a3r.at[n], r.rs_s.at[0, 2], r.rs_r.at[0, 2], zh=hp, zl=lp)
 
-    value_scores(2)
     take_bytes(r.b2r, r.rs_r.at[1, 1])
     for zp in range(2):
         total = r.b2s[x, zp].astype(F32)
@@ -462,35 +462,34 @@
     factor = 1.0 / math.sqrt(TOKEN_COUNT)
     here_x, here_zl = c * 4 + x, c * 4 + zl
 
+    def spread(src, dst, part, axis, at):
+        target = 0 if part == 0 else 1
+        for d in range(1, 4):
+            where = {axis: turned(at, d, 4), "c": target}
+            send(src, dst, r.rs_s.at[part, 3], r.rs_r.at[part, 3], **where)
+
+        @pl.when(c != target)
+        def _():
+            send(src, dst, r.rs_s.at[part, 3], r.rs_r.at[part, 3], c=target)
+
+    take_bytes(r.a3r, r.rs_r.at[0, 2])
+    total = r.a3s[zh].astype(F32)
+    for d in range(7):
+        total = total + r.a3r[d].astype(F32)
+    r.fa[...] = total * factor
+    spread(r.fa, r.wga.at[here_x], 0, "x", x)
     take_bytes(r.c3r, r.rs_r.at[2, 2])
     total = r.c3s[...].astype(F32)
     for d in range(3):
         total = total + r.c3r[d].astype(F32)
     r.fc[...] = total * factor
+    spread(r.fc, r.wgc.at[here_zl], 2, "zl", zl)
     take_bytes(r.b3r, r.rs_r.at[1, 2])
     total = r.b3s[zh].astype(F32)
     for d in range(7):
         total = total + r.b3r[d].astype(F32)
     r.fb[...] = total * factor
-    take_bytes(r.a3r, r.rs_r.at[0, 2])
-    total = r.a3s[zh].astype(F32)
-    for d in range(7):
-        total = total + r.a3r[d].astype(F32)
-    r.fa[...] = total * factor
-
-    def spread(src, dst, part, axis, at):
-        target = 0 if part == 0 else 1
-        for d in range(1, 4):
-            where = {axis: turned(at, d, 4), "c": target}
-            send(src, dst, r.rs_s.at[part, 3], r.rs_r.at[part, 3], **where)
-
-        @pl.when(c != target)
-        def _():
-            send(src, dst, r.rs_s.at[part, 3], r.rs_r.at[part, 3], c=target)
-
-    spread(r.fa, r.wga.at[here_x], 0, "x", x)
     spread(r.fb, r.wgb.at[here_x], 1, "x", x)
-    spread(r.fc, r.wgc.at[here_zl], 2, "zl", zl)
 
     state_wait(1)
 

time: 57.4 us -> 56.9 us (level)
  no operation moved by 1% of the time
where the time goes in v4:
time: 56.9 us; the launch traced here: 56.7 us
  Pallas kernels  56.1 us (99%)
  between operations  0.64 us (1%)
    pallas_call x1, Pallas kernels, body(): pl.pallas_call(kernel, out_shape=tuple((jax.ShapeDtypeStruct(*spec) for s...  54.8 us
    pallas_call x1, Pallas kernels, body(): pl.pallas_call(put_out, out_shape=tuple((jax.ShapeDtypeStruct(*spec) for...  1.28 us

profile of v4, /device:TPU:1, one launch (start us, length us, event | category | flops | bytes accessed | tf_op | source)
XLA Modules:
  0.0 56.7 jit_solution(7466815971019235050)
XLA Ops:
  0.6 54.8 %shard_map.84 = (bf16[192,2048]{1,0:T(8,128)(2,1)S(1)}, bf16[192,512]{1,0:T(8,128)(2,1)S(1)}, bf16[192,2048]{1,0:T(8,128)(2,1)S(1)}, f32[64,512]{1,0:T(8,128)S(1)}) custom-call(bf16[192,2048]{1,0:T(8,128)(2,1)} %bitcast.7, bf16[192,2048]{1,0:T(8,128)(2,1)} %bitcast.8, bf16[192,512]{1,0:T(8,128)(2,1)} %bitcast.10, bf16[64,512]{1,0:T(8,128)(2,1)} %w_h.1, ...), custom_call_target="tpu_custom_call" | custom-call | tf_op jit(solution)/shard_map/pallas_call | solution.py:571
  55.5 1.3 %shard_map.85 = (bf16[192,2048]{1,0:T(8,128)(2,1)}, bf16[192,512]{1,0:T(8,128)(2,1)}, bf16[192,2048]{1,0:T(8,128)(2,1)}, f32[64,512]{1,0:T(8,128)}) custom-call(bf16[192,2048]{1,0:T(8,128)(2,1)S(1)} %get-tuple-element.12.refs_0_, bf16[192,512]{1,0:T(8,128)(2,1)S(1)} %get-tuple-element.13.refs_1_, bf16[192,2048]{1,0:T(8,128)(2,1)S(1)} %get-tuple-element.14.refs_2_, ...), custom_call_target="tpu_custom_call" | custom-call | tf_op jit(solution)/shard_map/pallas_call | solution.py:587

commit v5 on v4

--- a/solution.py
+++ b/solution.py
@@ -21,6 +21,8 @@
 F32 = jnp.float32
 MESH = pl.DeviceIdType.MESH
 TOKEN_COUNT = 98304
+FAR_FIRST_4 = (2, 1, 3)
+FAR_FIRST_8 = (4, 3, 5, 2, 6, 1, 7)
 
 OUTS = dict(
     qgo=((TOKENS, WIDTH), BF),
@@ -179,7 +181,7 @@
     row_sum, row_sums = (r.st_t0, r.st_t1), (r.st_r20, r.st_r21)
 
     def state_first(i):
-        for d in range(1, 4):
+        for d in FAR_FIRST_4:
             xp = turned(x, d, 4)
             send(r.st_s.at[i, xp], r.st_r1.at[i, x], r.st_ss.at[i, 0], r.st_rs.at[i, 0], x=xp)
         r.st_r1[i, x] = r.st_s[i, x]
@@ -204,7 +206,7 @@
             for p in range(xp + 1, 4) if i == 0 else range(xp):
                 value = value + r.st_r1[i, p]
             r.st_o[i, xp] = value.astype(BF)
-        for d in range(1, 4):
+        for d in FAR_FIRST_4:
             xp = turned(x, d, 4)
             send(r.st_o.at[i, xp], r.st_r3.at[i, x], r.st_ss.at[i, 2], r.st_rs.at[i, 2], x=xp)
         r.st_r3[i, x] = r.st_o[i, x]
@@ -236,10 +238,10 @@
             for way in ways:
                 piece = shard_at(j, turned(y, 8 - step if way == 0 else step, 8), h)
                 take_bytes(piece, r.wr_r.at[way, j, step - 1 + 4 * h])
+                if step == 2 and way == j:
+                    along(way, j, 4, h, piece, 2)
                 if step < 3:
                     along(way, j, step + 1, h, piece)
-                if step == 2 and way == j:
-                    along(way, j, 4, h, piece, 2)
                 to_partner(j, piece)
 
     for edge, targets in ((3, (1, 0)), (0, (2, 3))):
@@ -334,15 +336,20 @@
                 r.gb[yp, zp, u] = part[64 + 16 * u : 80 + 16 * u, :128]
                 r.gc[zp, u, yp] = part[64 + 16 * u : 80 + 16 * u, 128:]
 
-    z_peers = [(dh, dl) for dh in range(2) for dl in range(4)][1:]
-    for d in range(1, 4):
+    z = zh * 4 + zl
+
+    def z_at(d):
+        place = turned(z, d, 8)
+        return lax.div(place, 4), lax.rem(place, 4)
+
+    for d in FAR_FIRST_4:
         xp = turned(x, d, 4)
         send(r.ga.at[xp], r.a1.at[d - 1], r.rs_s.at[0, 0], r.rs_r.at[0, 0], x=xp)
-    for n, (dh, dl) in enumerate(z_peers):
-        hp, lp = turned(zh, dh, 2), turned(zl, dl, 4)
-        send(r.gc.at[hp, lp], r.c1.at[n], r.rs_s.at[2, 0], r.rs_r.at[2, 0], zh=hp, zl=lp)
-
-    for d in range(1, 8):
+    for d in FAR_FIRST_8:
+        hp, lp = z_at(d)
+        send(r.gc.at[hp, lp], r.c1.at[d - 1], r.rs_s.at[2, 0], r.rs_r.at[2, 0], zh=hp, zl=lp)
+
+    for d in FAR_FIRST_8:
         yp = turned(y, d, 8)
         send(r.gb.at[yp], r.b1.at[d - 1], r.rs_s.at[1, 0], r.rs_r.at[1, 0], y=yp)
     relay(4, 0, (0,))
@@ -357,7 +364,7 @@
             total = total + r.a1[d, yp].astype(F32)
         r.a2s[yp] = total.astype(BF)
 
-    for d in range(1, 8):
+    for d in FAR_FIRST_8:
         yp = turned(y, d, 8)
         send(r.a2s.at[yp], r.a2r.at[d - 1], r.rs_s.at[0, 1], r.rs_r.at[0, 1], y=yp)
 
@@ -401,7 +408,7 @@
             for d in range(7):
                 total = total + r.b1[d, zp, u].astype(F32)
             r.b2s[u, zp] = total.astype(BF)
-    for d in range(1, 4):
+    for d in FAR_FIRST_4:
         xp = turned(x, d, 4)
         send(r.b2s.at[xp], r.b2r.at[d - 1], r.rs_s.at[1, 1], r.rs_r.at[1, 1], x=xp)
 
@@ -411,7 +418,7 @@
         for d in range(7):
             total = total + r.c1[d, yp].astype(F32)
         r.c2s[yp] = total.astype(BF)
-    for d in range(1, 8):
+    for d in FAR_FIRST_8:
         yp = turned(y, d, 8)
         send(r.c2s.at[yp], r.c2r.at[d - 1], r.rs_s.at[2, 1], r.rs_r.at[2, 1], y=yp)
 
@@ -425,9 +432,9 @@
         for d in range(7):
             total = total + r.a2r[d, zp].astype(F32)
         r.a3s[zp] = total.astype(BF)
-    for n, (dh, dl) in enumerate(z_peers):
-        hp, lp = turned(zh, dh, 2), turned(zl, dl, 4)
-        send(r.a3s.at[hp], r.a3r.at[n], r.rs_s.at[0, 2], r.rs_r.at[0, 2], zh=hp, zl=lp)
+    for d in FAR_FIRST_8:
+        hp, lp = z_at(d)
+        send(r.a3s.at[hp], r.a3r.at[d - 1], r.rs_s.at[0, 2], r.rs_r.at[0, 2], zh=hp, zl=lp)
 
     take_bytes(r.b2r, r.rs_r.at[1, 1])
     for zp in range(2):
@@ -435,16 +442,16 @@
         for d in range(3):
             total = total + r.b2r[d, zp].astype(F32)
         r.b3s[zp] = total.astype(BF)
-    for n, (dh, dl) in enumerate(z_peers):
-        hp, lp = turned(zh, dh, 2), turned(zl, dl, 4)
-        send(r.b3s.at[hp], r.b3r.at[n], r.rs_s.at[1, 2], r.rs_r.at[1, 2], zh=hp, zl=lp)
+    for d in FAR_FIRST_8:
+        hp, lp = z_at(d)
+        send(r.b3s.at[hp], r.b3r.at[d - 1], r.rs_s.at[1, 2], r.rs_r.at[1, 2], zh=hp, zl=lp)
 
     take_bytes(r.c2r, r.rs_r.at[2, 1])
     total = r.c2s[y].astype(F32)
     for d in range(7):
         total = total + r.c2r[d].astype(F32)
     r.c3s[...] = total.astype(BF)
-    for d in range(1, 4):
+    for d in FAR_FIRST_4:
         xp = turned(x, d, 4)
         send(r.c3s, r.c3r.at[d - 1], r.rs_s.at[2, 2], r.rs_r.at[2, 2], x=xp)
 
@@ -464,7 +471,7 @@
 
     def spread(src, dst, part, axis, at):
         target = 0 if part == 0 else 1
-        for d in range(1, 4):
+        for d in FAR_FIRST_4:
             where = {axis: turned(at, d, 4), "c": target}
             send(src, dst, r.rs_s.at[part, 3], r.rs_r.at[part, 3], **where)
 

time: 56.9 us -> 54.8 us (0.963)
  Pallas kernels: 56.1 us -> 54 us
    pallas_call x1, Pallas kernels: 54.8 us -> 52.8 us  [body(): pl.pallas_call(kernel, out_shape=tuple((jax.ShapeDtypeStruct(*spec) for s...]
where the time goes in v5:
time: 54.8 us; the launch traced here: 54.7 us
  Pallas kernels  54 us (99%)
  between operations  0.64 us (1%)
    pallas_call x1, Pallas kernels, body(): pl.pallas_call(kernel, out_shape=tuple((jax.ShapeDtypeStruct(*spec) for s...  52.8 us
    pallas_call x1, Pallas kernels, body(): pl.pallas_call(put_out, out_shape=tuple((jax.ShapeDtypeStruct(*spec) for...  1.28 us

profile of v5, /device:TPU:1, one launch (start us, length us, event | category | flops | bytes accessed | tf_op | source)
XLA Modules:
  0.0 54.7 jit_solution(11274489467025424429)
XLA Ops:
  0.6 52.8 %shard_map.84 = (bf16[192,2048]{1,0:T(8,128)(2,1)S(1)}, bf16[192,512]{1,0:T(8,128)(2,1)S(1)}, bf16[192,2048]{1,0:T(8,128)(2,1)S(1)}, f32[64,512]{1,0:T(8,128)S(1)}) custom-call(bf16[192,2048]{1,0:T(8,128)(2,1)} %bitcast.7, bf16[192,2048]{1,0:T(8,128)(2,1)} %bitcast.8, bf16[192,512]{1,0:T(8,128)(2,1)} %bitcast.10, bf16[64,512]{1,0:T(8,128)(2,1)} %w_h.1, ...), custom_call_target="tpu_custom_call" | custom-call | tf_op jit(solution)/shard_map/pallas_call | solution.py:578
  53.4 1.3 %shard_map.85 = (bf16[192,2048]{1,0:T(8,128)(2,1)}, bf16[192,512]{1,0:T(8,128)(2,1)}, bf16[192,2048]{1,0:T(8,128)(2,1)}, f32[64,512]{1,0:T(8,128)}) custom-call(bf16[192,2048]{1,0:T(8,128)(2,1)S(1)} %get-tuple-element.12.refs_0_, bf16[192,512]{1,0:T(8,128)(2,1)S(1)} %get-tuple-element.13.refs_1_, bf16[192,2048]{1,0:T(8,128)(2,1)S(1)} %get-tuple-element.14.refs_2_, ...), custom_call_target="tpu_custom_call" | custom-call | tf_op jit(solution)/shard_map/pallas_call | solution.py:594

commit v6 on v5

--- a/solution.py
+++ b/solution.py
@@ -39,6 +39,7 @@
     k=((TOKENS, KV_WIDTH), BF),
     kt=((KV_WIDTH, TOKENS), BF),
     v=((TOKENS, KV_WIDTH), BF),
+    vf=((TOKENS, KV_WIDTH), F32),
     wb=((32, 64, KV_WIDTH), BF),
     vgi=((TOKENS, KV_WIDTH), F32),
     vg=((2, TOKENS, 256), BF),
@@ -190,7 +191,7 @@
         take_bytes(r.st_r1.at[i, pl.ds(0, 3)], r.st_rs.at[i, 0])
         total = sum(r.st_r1[i, p] for p in range(4)).astype(row_sum[i].dtype)
         row_sum[i][...] = total
-        for d in range(1, 4):
+        for d in (1, 2, 3) if i == 0 else (3, 2, 1):
             zp = turned(zl, d, 4)
             send(row_sum[i], row_sums[i].at[zl], r.st_ss.at[i, 1], r.st_rs.at[i, 1], zl=zp)
         row_sums[i][zl] = total
@@ -304,10 +305,10 @@
         take_bytes(shard_at(1, y, h), r.wz_r.at[h])
         begin(1, h)
     transpose(r.x, r.xt, 0, 16)
-    relay(2, 0)
     take_bytes(r.x2, r.xx_r.at[0])
     transpose(r.x2, r.x2t, 0, 16)
     state_third(0)
+    relay(2, 0)
     relay(1, 1)
     state_wait(0)
 
@@ -356,6 +357,13 @@
     relay(3, 1)
     relay(4, 1, (1,))
 
+    def values_part(row):
+        half = r.wb[pl.ds(row * 16, 16)].reshape(WIDTH // 2, KV_WIDTH)
+        return dot(r.x[:, span(row * 1024, 1024)], half)
+
+    take_bytes(r.wb.at[pl.ds(0, 8)], r.wd_r.at[0])
+    r.vf[...] = values_part(zh)
+
     take_bytes(r.a1, r.rs_r.at[0, 0])
 
     for yp in range(8):
@@ -368,10 +376,8 @@
         yp = turned(y, d, 8)
         send(r.a2s.at[yp], r.a2r.at[d - 1], r.rs_s.at[0, 1], r.rs_r.at[0, 1], y=yp)
 
-    take_bytes(r.wb.at[pl.ds(0, 8)], r.wd_r.at[0])
     take_bytes(r.wb.at[pl.ds(0, 8)], r.wd_r.at[1])
-    whole = r.wb[...].reshape(WIDTH, KV_WIDTH)
-    r.v[...] = dot(r.x[...], whole).astype(BF)
+    r.v[...] = (r.vf[...] + values_part(1 - zh)).astype(BF)
     for p in range(4):
         cols = slice(p * 128, p * 128 + 128)
         m = dot(r.v[:, cols], r.k[:, cols], ((0,), (0,)))

time: 54.8 us -> 54.9 us (level)
  no operation moved by 1% of the time
where the time goes in v6:
time: 54.9 us; the launch traced here: 54.8 us
  Pallas kernels  54.1 us (99%)
  between operations  0.64 us (1%)
    pallas_call x1, Pallas kernels, body(): pl.pallas_call(kernel, out_shape=tuple((jax.ShapeDtypeStruct(*spec) for s...  52.9 us
    pallas_call x1, Pallas kernels, body(): pl.pallas_call(put_out, out_shape=tuple((jax.ShapeDtypeStruct(*spec) for...  1.28 us

profile of v6, /device:TPU:1, one launch (start us, length us, event | category | flops | bytes accessed | tf_op | source)
XLA Modules:
  0.0 54.8 jit_solution(9461021497627136550)
XLA Ops:
  0.6 52.9 %shard_map.84 = (bf16[192,2048]{1,0:T(8,128)(2,1)S(1)}, bf16[192,512]{1,0:T(8,128)(2,1)S(1)}, bf16[192,2048]{1,0:T(8,128)(2,1)S(1)}, f32[64,512]{1,0:T(8,128)S(1)}) custom-call(bf16[192,2048]{1,0:T(8,128)(2,1)} %bitcast.7, bf16[192,2048]{1,0:T(8,128)(2,1)} %bitcast.8, bf16[192,512]{1,0:T(8,128)(2,1)} %bitcast.10, bf16[64,512]{1,0:T(8,128)(2,1)} %w_h.1, ...), custom_call_target="tpu_custom_call" | custom-call | tf_op jit(solution)/shard_map/pallas_call | solution.py:584
  53.5 1.3 %shard_map.85 = (bf16[192,2048]{1,0:T(8,128)(2,1)}, bf16[192,512]{1,0:T(8,128)(2,1)}, bf16[192,2048]{1,0:T(8,128)(2,1)}, f32[64,512]{1,0:T(8,128)}) custom-call(bf16[192,2048]{1,0:T(8,128)(2,1)S(1)} %get-tuple-element.12.refs_0_, bf16[192,512]{1,0:T(8,128)(2,1)S(1)} %get-tuple-element.13.refs_1_, bf16[192,2048]{1,0:T(8,128)(2,1)S(1)} %get-tuple-element.14.refs_2_, ...), custom_call_target="tpu_custom_call" | custom-call | tf_op jit(solution)/shard_map/pallas_call | solution.py:600

commit v7 on v6

--- a/solution.py
+++ b/solution.py
@@ -191,7 +191,7 @@
         take_bytes(r.st_r1.at[i, pl.ds(0, 3)], r.st_rs.at[i, 0])
         total = sum(r.st_r1[i, p] for p in range(4)).astype(row_sum[i].dtype)
         row_sum[i][...] = total
-        for d in (1, 2, 3) if i == 0 else (3, 2, 1):
+        for d in range(1, 4):
             zp = turned(zl, d, 4)
             send(row_sum[i], row_sums[i].at[zl], r.st_ss.at[i, 1], r.st_rs.at[i, 1], zl=zp)
         row_sums[i][zl] = total
@@ -305,10 +305,10 @@
         take_bytes(shard_at(1, y, h), r.wz_r.at[h])
         begin(1, h)
     transpose(r.x, r.xt, 0, 16)
+    relay(2, 0)
     take_bytes(r.x2, r.xx_r.at[0])
     transpose(r.x2, r.x2t, 0, 16)
     state_third(0)
-    relay(2, 0)
     relay(1, 1)
     state_wait(0)
 

time: 54.9 us -> 54.6 us (level)
  no operation moved by 1% of the time
where the time goes in v7:
time: 54.6 us; the launch traced here: 54.5 us
  Pallas kernels  53.8 us (99%)
  between operations  0.64 us (1%)
    pallas_call x1, Pallas kernels, body(): pl.pallas_call(kernel, out_shape=tuple((jax.ShapeDtypeStruct(*spec) for s...  52.6 us
    pallas_call x1, Pallas kernels, body(): pl.pallas_call(put_out, out_shape=tuple((jax.ShapeDtypeStruct(*spec) for...  1.28 us

profile of v7, /device:TPU:1, one launch (start us, length us, event | category | flops | bytes accessed | tf_op | source)
XLA Modules:
  0.0 54.5 jit_solution(9085203052539939042)
XLA Ops:
  0.6 52.6 %shard_map.84 = (bf16[192,2048]{1,0:T(8,128)(2,1)S(1)}, bf16[192,512]{1,0:T(8,128)(2,1)S(1)}, bf16[192,2048]{1,0:T(8,128)(2,1)S(1)}, f32[64,512]{1,0:T(8,128)S(1)}) custom-call(bf16[192,2048]{1,0:T(8,128)(2,1)} %bitcast.7, bf16[192,2048]{1,0:T(8,128)(2,1)} %bitcast.8, bf16[192,512]{1,0:T(8,128)(2,1)} %bitcast.10, bf16[64,512]{1,0:T(8,128)(2,1)} %w_h.1, ...), custom_call_target="tpu_custom_call" | custom-call | tf_op jit(solution)/shard_map/pallas_call | solution.py:584
  53.2 1.3 %shard_map.85 = (bf16[192,2048]{1,0:T(8,128)(2,1)}, bf16[192,512]{1,0:T(8,128)(2,1)}, bf16[192,2048]{1,0:T(8,128)(2,1)}, f32[64,512]{1,0:T(8,128)}) custom-call(bf16[192,2048]{1,0:T(8,128)(2,1)S(1)} %get-tuple-element.12.refs_0_, bf16[192,512]{1,0:T(8,128)(2,1)S(1)} %get-tuple-element.13.refs_1_, bf16[192,2048]{1,0:T(8,128)(2,1)S(1)} %get-tuple-element.14.refs_2_, ...), custom_call_target="tpu_custom_call" | custom-call | tf_op jit(solution)/shard_map/pallas_call | solution.py:600
